TPU v7x, 32 devices: a whole 2x2x4 slice. The times are simulated.
32 devices in a mesh: outer: 4 (over z), middle: 2 (over y), inner: 4 (over x, core).
Axes of the slice: x: 2, y: 2, z: 4, core: 2. Of those that a mesh axis runs over, the one named last changes fastest.
Arguments:
- g_embed: float32 [32, 32768, 128], P(('outer', 'middle', 'inner'))
- g_attn: float32 [32, 16, 128, 512], P(('outer', 'middle', 'inner'))
- g_ffn_in: float32 [32, 16, 128, 512], P(('outer', 'middle', 'inner'))
- g_ffn_out: float32 [32, 16, 512, 128], P(('outer', 'middle', 'inner'))
- g_vec: float32 [32, 16, 1664], P(('outer', 'middle', 'inner'))
- m_flat: float32 [7366656], P(('outer', 'middle', 'inner'))
- v_flat: float32 [7366656], P(('outer', 'middle', 'inner'))
- w_flat: float32 [7366656], P(('outer', 'middle', 'inner'))
Outputs:
- output 1: float32 [7366656], P(('outer', 'middle', 'inner'))
- output 2: float32 [7366656], P(('outer', 'middle', 'inner'))
- output 3: float32 [7366656], P(('outer', 'middle', 'inner'))
- output 4: bfloat16 [32768, 128], replicated
- output 5: bfloat16 [16, 128, 512], replicated
- output 6: bfloat16 [16, 128, 512], replicated
- output 7: bfloat16 [16, 512, 128], replicated
- output 8: bfloat16 [16, 1664], replicated
- output 9: bfloat16 [32, 460416], P(('outer', 'middle', 'inner'))
All inputs are finite; a program needn't handle non-finite values.
Results may differ from a plain program's by a relative error of at most 0.001.
Values are sent between devices in bfloat16 or wider.
A program may use at most 1 GiB of HBM per device.

v0:
```python
import math
import jax
import jax.numpy as jnp
from jax import lax
from jax.sharding import PartitionSpec as P

MESH_AXES = ('outer', 'middle', 'inner')
ADAM_BETA1 = 0.9
ADAM_BETA2 = 0.98
ADAM_EPS = 1e-9
LEARN_RATE = 0.05
ADAM_STEP = 3


def adam_update(grad_mean, m_old, v_old, w_old):
    m_new = ADAM_BETA1 * m_old + (1.0 - ADAM_BETA1) * grad_mean
    v_new = ADAM_BETA2 * v_old + (1.0 - ADAM_BETA2) * (grad_mean * grad_mean)
    m_hat = m_new / (1.0 - ADAM_BETA1 ** ADAM_STEP)
    v_hat = v_new / (1.0 - ADAM_BETA2 ** ADAM_STEP)
    w_new = w_old - LEARN_RATE * m_hat / (jnp.sqrt(v_hat) + ADAM_EPS)
    return m_new, v_new, w_new


def split_tensors(flat_values, shape_list):
    pieces = []
    offset = 0
    for shape in shape_list:
        count = math.prod(shape)
        pieces.append(flat_values[offset:offset + count].reshape(shape))
        offset += count
    return pieces


def own_chip_block(w_tensors, chip_index, num_chips):
    embed_rows = w_tensors[0].shape[0] // num_chips
    block_list = [lax.dynamic_slice_in_dim(w_tensors[0], chip_index * embed_rows, embed_rows, axis=0).reshape(-1)]
    for tensor in w_tensors[1:]:
        block_rows = tensor.shape[1] // num_chips
        block_list.append(lax.dynamic_slice_in_dim(tensor, chip_index * block_rows, block_rows, axis=1).reshape(-1))
    return jnp.concatenate(block_list)[None, :]


def solution(mesh):
    num_devices = mesh.shape['outer'] * mesh.shape['middle'] * mesh.shape['inner']
    num_chips = num_devices // 2

    def local_step(g_embed, g_attn, g_ffn_in, g_ffn_out, g_vec, m_shard, v_shard, w_shard):
        grad_list = (g_embed, g_attn, g_ffn_in, g_ffn_out, g_vec)
        local_flat = jnp.concatenate([gradient.reshape(-1) for gradient in grad_list])
        grad_mean = lax.psum_scatter(local_flat, MESH_AXES, scatter_dimension=0, tiled=True) / num_devices
        m_new, v_new, w_new = adam_update(grad_mean, m_shard, v_shard, w_shard)
        w_full = lax.all_gather(w_new.astype(jnp.bfloat16), MESH_AXES, axis=0, tiled=True)
        w_tensors = split_tensors(w_full, [gradient.shape[1:] for gradient in grad_list])
        device_index = (lax.axis_index('outer') * mesh.shape['middle'] + lax.axis_index('middle')) * mesh.shape['inner'] + lax.axis_index('inner')
        w_chip = own_chip_block(w_tensors, device_index // 2, num_chips)
        return (m_new, v_new, w_new) + tuple(w_tensors) + (w_chip,)

    return jax.shard_map(local_step, mesh=mesh, in_specs=(P(MESH_AXES),) * 8, out_specs=(P(MESH_AXES),) * 3 + (P(),) * 5 + (P(MESH_AXES),), check_vma=False)
```

profile of v0, /device:TPU:0, one launch (start us, length us, event | category | flops | bytes accessed | tf_op | source)
XLA Modules:
  0.0 794.6 jit_solution(12934854281022799839)
XLA Ops:
  7.2 0.0 all-reduce.7.cloned.1.call-start
  7.2 0.0 copy-start.1
  7.2 0.0 copy-start.2
  7.2 13.1 %bitcast_dynamic-update-slice_fusion = f32[7366656]{0:T(1024)} fusion(f32[1,32768,128]{2,1,0:T(8,128)} %param.8), kind=kLoop, calls=%fused_computation | loop fusion | bytes 33554432
  20.3 0.0 copy-start.7
  20.3 0.0 copy-done.1
  20.3 3.1 copy.17
  23.4 0.0 copy-done.2
  23.4 3.0 copy.18
  26.4 0.0 copy-done.7
  26.5 0.0 copy-start.3
  26.5 4.6 constant_dynamic-update-slice_fusion.3
  31.0 4.4 constant_dynamic-update-slice_fusion.2
  35.5 0.0 copy-done.3
  35.5 2.2 constant_dynamic-update-slice_fusion.1
  37.7 0.6 constant_dynamic-update-slice_fusion
  38.3 0.0 copy-start.4
  38.3 0.0 copy-start.5
  38.3 0.0 copy-start.6
  38.3 0.0 all-reduce.7.cloned.1.call-update
  38.4 0.0 all-reduce.5.cloned.1.call-start
  38.4 446.9 %all-reduce.7.cloned.1.call-done = f32[7366656]{0:T(1024)} async-done(((f32[7366656]{0:T(1024)}), f32[7366656]{0:T(1024)}) %all-reduce.7.cloned.1.call-update) | async-done | bytes 29466640
  485.3 0.0 copy-done.4
  485.3 0.0 copy-done.5
  485.3 0.0 copy-done.6
  485.3 3.5 fusion
  488.9 5.3 broadcast.6
  494.2 8.2 %dynamic-update-slice = bf16[7366656]{0:T(1024)(128)(2,1)} dynamic-update-slice(bf16[7366656]{0:T(1024)(128)(2,1)} %broadcast.6, bf16[230208]{0:T(1024)(128)(2,1)S(1)} %get-tuple-element.9, u32[]{:T(128)S(6)} %multiply.8) | dynamic-update-slice | bytes 920836
  502.4 0.0 all-reduce.5.cloned.1.call-update
  502.4 255.0 %all-reduce.5.cloned.1.call-done = bf16[7366656]{0:T(1024)(128)(2,1)} async-done(((bf16[7366656]{0:T(1024)(128)(2,1)}), bf16[7366656]{0:T(1024)(128)(2,1)}) %all-reduce.5.cloned.1.call-update) | async-done | bytes 14733328
  757.4 0.0 slice-start
  757.4 5.3 fusion.1
  762.7 4.3 reshape.74
  767.0 2.5 reshape.75
  769.6 0.0 slice-done
  769.6 0.1 reshape.77
  769.7 0.0 copy-start.8
  769.7 1.0 dynamic-slice_bitcast_fusion
  770.7 0.1 copy.19
  770.7 0.1 copy.20
  770.8 0.1 constant_dynamic-slice_fusion
  770.9 0.1 reshape.82
  771.0 4.2 slice_bitcast_fusion
  775.2 0.0 copy-start
  775.3 1.1 constant_dynamic-slice_fusion.1
  776.5 11.3 %broadcast_in_dim.3 = bf16[1,460416]{1,0:T(2,128)(2,1)} reshape(bf16[460416]{0:T(1024)(128)(2,1)S(1)} %constant_dynamic-update-slice_fusion.4) | data formatting | bytes 1841664 | tf_op jit(solution)/shard_map/broadcast_in_dim | solution.py:40
  787.7 0.0 copy-done.8
  787.7 0.0 copy-done
  (6 shorter events, 0.1 us)
Async XLA Ops:
  7.2 478.1 %all-reduce.7.cloned.1.call-start = ((), (), s32[]{:S(2)}) async-start(), calls=%async_computation.1 | async-start | bytes 58933248
  7.2 13.1 %copy-start.1 = (f32[1,16,128,512]{3,2,1,0:T(8,128)S(1)}, f32[1,16,128,512]{3,2,1,0:T(8,128)}, u32[]{:S(2)}) copy-start(f32[1,16,128,512]{3,2,1,0:T(8,128)} %param.9) | copy-start | bytes 12582916
  7.2 16.2 %copy-start.2 = (f32[1,16,128,512]{3,2,1,0:T(8,128)S(1)}, f32[1,16,128,512]{3,2,1,0:T(8,128)}, u32[]{:S(2)}) copy-start(f32[1,16,128,512]{3,2,1,0:T(8,128)} %param.10) | copy-start | bytes 12582916
  20.3 6.1 copy-start.7
  26.5 9.0 %copy-start.3 = (f32[1,16,512,128]{3,2,1,0:T(8,128)S(1)}, f32[1,16,512,128]{3,2,1,0:T(8,128)}, u32[]{:S(2)}) copy-start(f32[1,16,512,128]{3,2,1,0:T(8,128)} %param.11) | copy-start | bytes 12582916
  38.3 447.0 %copy-start.4 = (f32[230208]{0:T(1024)S(1)}, f32[230208]{0:T(1024)}, u32[]{:S(2)}) copy-start(f32[230208]{0:T(1024)} %param.15) | copy-start | bytes 2762500
  38.3 447.0 %copy-start.5 = (f32[230208]{0:T(1024)S(1)}, f32[230208]{0:T(1024)}, u32[]{:S(2)}) copy-start(f32[230208]{0:T(1024)} %param.14) | copy-start | bytes 2762500
  38.3 447.0 %copy-start.6 = (f32[230208]{0:T(1024)S(1)}, f32[230208]{0:T(1024)}, u32[]{:S(2)}) copy-start(f32[230208]{0:T(1024)} %param.13) | copy-start | bytes 2762500
  38.4 719.0 %all-reduce.5.cloned.1.call-start = ((), (), s32[]{:S(2)}) async-start(), calls=%async_computation | async-start | bytes 29466624
  757.4 12.2 %slice-start = ((bf16[7366656]{0:T(1024)(128)(2,1)}), bf16[26624]{0:T(1024)(128)(2,1)S(1)}, s32[]{:S(2)}) async-start(bf16[7366656]{0:T(1024)(128)(2,1)} %all-reduce.5.cloned.1.call-done), calls=%async_computation.2 | async-start | bytes 106496 | tf_op jit(solution)/shard_map/slice | solution.py:29
  769.7 18.1 %copy-start.8 = (bf16[16,1664]{1,0:T(8,128)(2,1)}, bf16[16,1664]{1,0:T(8,128)(2,1)S(1)}, u32[]{:S(2)}) copy-start(bf16[16,1664]{1,0:T(8,128)(2,1)S(1)} %reshape.77) | copy-start | bytes 159748
  775.2 12.5 %copy-start = (bf16[32768,128]{1,0:T(8,128)(2,1)}, bf16[32768,128]{1,0:T(8,128)(2,1)S(1)}, u32[]{:S(2)}) copy-start(bf16[32768,128]{1,0:T(8,128)(2,1)S(1)} %slice_bitcast_fusion) | copy-start | bytes 25165828
Sparse Core Ops, SparseCore 0:
  38.5 446.7 all-reduce.6
  502.5 254.8 all-reduce.4
where the time goes:
time: 796 us; the launch traced here: 795 us
  waiting for transfers between devices  702 us (88%)
  local copies, waits for them, and re-layouts  74.8 us (9%)
  between operations  14.2 us (2%)
    unnamed x4, waiting for transfers between devices  702 us
    unnamed x33, local copies, waits for them, and re-layouts  45.1 us
  transfers between devices with their start and end apart: 2, of which 2 were waited for; matrix products, arithmetic and copies ran while one was open for 0% of the time, Pallas kernels for 0%

commit v1 on v0

v1 whole, which is shorter than its diff:
```python
import jax
import jax.numpy as jnp
from jax import lax
from jax.experimental import pallas as pl
from jax.experimental.pallas import tpu as pltpu
from jax.sharding import PartitionSpec as P

MESH_AXES = ('outer', 'middle', 'inner')
MESH = pl.DeviceIdType.MESH
BETA1, BETA2, EPS, RATE, STEP = 0.9, 0.98, 1e-9, 0.05, 3

NDEV = 32
ROWS = 1856
HALF = ROWS // 2
SLICE = 230208
SLICE_ROWS = 1800
PAD = SLICE_ROWS * 128 - SLICE
MARGIN = 64
COVER = ROWS + 8
TENSOR_ROWS = (32768, 8192, 8192, 8192, 208)
STARTS = (0, 32768, 40960, 49152, 57344, 57552)
PERM_LO, PERM_HI = 32768, 49152
PIECES = (32, 64, 128, 128, 128, 128, 128, 128, 64)
LOADS = (32, 64, 128, 256, 448)
E_SLOTS = 9


def bounds(sizes):
    out, at = [], 0
    for n in sizes:
        out.append((at, n))
        at += n
    return out


PIECE = bounds(PIECES)
LOAD = bounds(LOADS)
LOAD_OF = [next(i for i, (a, n) in enumerate(LOAD) if a <= p < a + n) for p, _ in PIECE]
SPLIT = ((0, 0), (1, 0))


def start_row(d):
    return 55696 if d == NDEV - 1 else 32 * (3597 * d // 64)


def merge_row(d):
    return 32 * (3597 * d // 64)


def segments(row, n):
    out = []
    for t in range(5):
        lo, hi = max(row, STARTS[t]), min(row + n, STARTS[t + 1])
        if lo < hi:
            out.append((t, lo - STARTS[t], lo - row, hi - lo))
    return out


def slot_of(color, k):
    x, y, z0, z1 = k % 2, k // 2 % 2, k // 4 % 2, k // 8
    return (x * 8 + z0 * 4 + y * 2 + z1) if color == 0 else (y * 8 + z0 * 4 + x * 2 + z1)


def event_order():
    unit = 128 * 4 / 46.6e3
    last = {0: 0.0}
    events, links = [], {'x': 0.0, 'y': 0.0, 'z': 0.0}
    heap = []
    loaded = 2.0
    load_done = []
    for a, n in LOAD:
        for color in (0, 1):
            loaded += n * 16 * 128 * 4 / 600e3
        load_done.append(loaded)
    for p in range(len(PIECE)):
        for color in (0, 1):
            heap.append((load_done[LOAD_OF[p]], 0, p, color))
    names = (('x', 'z', 'y', 'z'), ('y', 'z', 'x', 'z'))
    while heap:
        heap.sort()
        time, stage, p, color = heap.pop(0)
        events.append((stage, p, color))
        n = PIECE[p][1]
        if stage < 4:
            link, size = names[color][stage], n * (8 >> stage) * unit
        elif stage < 8:
            link, size = names[color][7 - stage], n * (1 << (stage - 4)) * unit / 2
        else:
            continue
        begin = max(time, links[link])
        links[link] = begin + size
        heap.append((begin + size + 3.0, stage + 1, p, color))
    return events


def big_kernel(ge, ga, gf1, gf2, gb, m_in, v_in, w_in, out_a, out_b, m_out, v_out, w_out, acc_a, acc_b, pair_a, pair_b, r1_a, r1_b, r2_a, r2_b, r3_a, r3_b, r4_a, r4_b, own_a, own_b, stage, cov, ld_sem, pr_recv, pr_send, rs_recv, rs_send, ag_recv, ag_send, loc_sem, dag_recv, dag_send, state_sem):
    grads = (ge, ga, gf1, gf2, gb)
    acc, pair, own, gat = (acc_a, acc_b), (pair_a, pair_b), (own_a, own_b), (out_a, out_b)
    rec = ((r1_a, r2_a, r3_a, r4_a), (r1_b, r2_b, r3_b, r4_b))
    z, y, inner = lax.axis_index('outer'), lax.axis_index('middle'), lax.axis_index('inner')
    x, c = inner // 2, inner % 2
    z0, z1 = z % 2, z // 2
    dev = (z * 2 + y) * 4 + inner
    to_pair = {'inner': inner + 1 - 2 * c}
    to_x = {'inner': inner + 2 - 4 * x}
    to_y = {'middle': 1 - y}
    to_z0 = {'outer': z + 1 - 2 * z0}
    to_z1 = {'outer': z + 2 - 4 * z1}
    routes = ((to_x, to_z0, to_y, to_z1), (to_y, to_z0, to_x, to_z1))
    bits = ((x, z0, y, z1), (y, z0, x, z1))

    barrier = pltpu.get_barrier_semaphore()
    for to in (to_pair, to_x, to_y, to_z0, to_z1):
        pl.semaphore_signal(barrier, inc=1, device_id=to, device_id_type=MESH)

    state_in = [pltpu.make_async_copy(src, stage.at[i, pl.ds(MARGIN, SLICE_ROWS)], state_sem.at[i]) for i, src in enumerate((m_in, v_in, w_in))]
    for copy in state_in:
        copy.start()
    pl.semaphore_wait(barrier, 5)

    def load_one(color, i, tensor, row, slot, at, n, mine):
        src = grads[tensor].at[pl.ds(row, n)]
        if mine:
            pltpu.make_async_copy(src, acc[color].at[slot, pl.ds(at, n)], ld_sem.at[color, i]).start()
        else:
            pltpu.make_async_remote_copy(src, pair[color].at[slot, pl.ds(at, n)], pr_send.at[color], pr_recv.at[color, i], device_id=to_pair, device_id_type=MESH).start()

    def load(i):
        at, n = LOAD[i]
        for color in (0, 1):
            @pl.loop(0, E_SLOTS)
            def _(k):
                slot = slot_of(color, k)
                for mine in (False, True):
                    d = 2 * k + (c if mine else 1 - c)
                    row = pl.multiple_of(32 * ((3597 * d) // 64), 32) + color * HALF + at
                    load_one(color, i, 0, row, slot, at, n, mine)
            for core in (0, 1):
                @pl.when(c == core)
                def _():
                    for k in range(E_SLOTS, NDEV // 2):
                        slot = slot_of(color, k)
                        for mine in (False, True):
                            d = 2 * k + (core if mine else 1 - core)
                            for tensor, row, off, rows in segments(start_row(d) + color * HALF + at, n):
                                load_one(color, i, tensor, row, slot, at + off, rows, mine)

    def wait_on(ref, sem):
        pltpu.make_async_copy(ref, ref, sem).wait()

    def add(color, into, slots, src, first, at, n):
        @pl.loop(0, slots)
        def _(i):
            acc[color][into + i, pl.ds(at, n), :] += src[first + i, pl.ds(at, n), :]

    def base(color, level):
        return sum((bits[color][i] * (8 >> i) for i in range(level)), 0 * c)

    def reduce_send(color, s, p):
        at, n = PIECE[p]
        size = 8 >> s
        first = base(color, s) + (1 - bits[color][s]) * size
        pltpu.make_async_remote_copy(acc[color].at[pl.ds(first, size), pl.ds(at, n)], rec[color][s].at[:, pl.ds(at, n)], rs_send.at[color, s], rs_recv.at[color, s, p], device_id=routes[color][s], device_id_type=MESH).start()

    def pair_out(color, slot, size, p):
        at, n = PIECE[p]
        block = gat[color].at[c, pl.ds(slot, size), pl.ds(at, n)]
        pltpu.make_async_remote_copy(block, block, dag_send.at[color], dag_recv.at[color], device_id=to_pair, device_id_type=MESH).start()

    def adam_block(g, load_state, store_state):
        g = g * (1.0 / NDEV)
        m = BETA1 * load_state(0) + (1.0 - BETA1) * g
        v = BETA2 * load_state(1) + (1.0 - BETA2) * (g * g)
        m_hat = m / (1.0 - BETA1 ** STEP)
        v_hat = v / (1.0 - BETA2 ** STEP)
        w = load_state(2) - RATE * m_hat / (jnp.sqrt(v_hat) + EPS)
        store_state(0, m)
        store_state(1, v)
        store_state(2, w)
        return w

    cover_start = jnp.where(dev == NDEV - 1, 55696, 32 * ((3597 * dev) // 64))

    def adam(color, p):
        at, n = PIECE[p]
        slot = base(color, 4)

        @pl.loop(0, n // 32)
        def _(j):
            r = pl.multiple_of(at + j * 32, 32)
            f = pl.multiple_of(color * HALF + r, 32)
            row = cover_start + f
            permuted = (row >= PERM_LO) & (row < PERM_HI)

            def group(index):
                for t in range(2):
                    parts = []
                    for q in (2 * t, 2 * t + 1):
                        where = index(f, q)

                        def keep(i, value, where=where):
                            cov[i, where, :] = value

                        parts.append(adam_block(acc[color][slot, pl.ds(r + 8 * q, 8), :], lambda i, where=where: cov[i, where, :], keep))
                    own[color][pl.ds(r + 16 * t, 16), :] = jnp.concatenate(parts, axis=0).astype(jnp.bfloat16)

            @pl.when(permuted)
            def _():
                group(lambda f, q: pl.ds(f + q, 8, stride=4))

            @pl.when(jnp.logical_not(permuted))
            def _():
                group(lambda f, q: pl.ds(f + 8 * q, 8))

    half_rows = jnp.where(dev == NDEV - 1, 115, (3597 * dev) % 64)
    shift = half_rows // 2
    lane = lax.broadcasted_iota(jnp.int32, (32, 128), 1)

    def moved(first, second):
        return jnp.where(lane < 64, pltpu.roll(first, 64, 1), pltpu.roll(second, 64, 1))

    def state_to_cover():
        for i, copy in enumerate(state_in):
            copy.wait()
            stage[i, 0:MARGIN, :] = jnp.zeros((MARGIN, 128), jnp.float32)
            stage[i, MARGIN + SLICE_ROWS:, :] = jnp.zeros((MARGIN, 128), jnp.float32)
            cov[i, ROWS:, :] = jnp.zeros((COVER - ROWS, 128), jnp.float32)

        @pl.loop(0, ROWS // 32)
        def _(j):
            f = pl.multiple_of(j * 32, 32)
            r = MARGIN + f - shift
            for i in range(3):
                here = stage[i, pl.ds(r, 32), :]
                before = stage[i, pl.ds(r - 1, 32), :]
                cov[i, pl.ds(f, 32), :] = jnp.where(c == 1, moved(before, here), here)

    def cover_to_state():
        @pl.loop(0, SLICE_ROWS // 8)
        def _(j):
            r = pl.multiple_of(j * 8, 8)
            for i in range(3):
                here = cov[i, pl.ds(r + shift, 8), :]
                after = cov[i, pl.ds(r + shift + 1, 8), :]
                both = jnp.where(lane[:8] < 64, pltpu.roll(here, 64, 1), pltpu.roll(after, 64, 1))
                stage[i, pl.ds(MARGIN + r, 8), :] = jnp.where(c == 1, both, here)

    load(0)
    load(1)
    events = event_order()
    loads_started = 2
    waited = set()
    state_ready = False
    for stage_no, p, color in events:
        at, n = PIECE[p]
        if stage_no == 0:
            i = LOAD_OF[p]
            while loads_started < min(i + 2, len(LOAD)):
                load(loads_started)
                loads_started += 1
            if (color, i) not in waited:
                waited.add((color, i))
                la, ln = LOAD[i]
                wait_on(acc[color].at[:, pl.ds(la, ln)], ld_sem.at[color, i])
                wait_on(pair[color].at[:, pl.ds(la, ln)], pr_recv.at[color, i])
            away, home = (1 - bits[color][0]) * 8, bits[color][0] * 8
            add(color, away, 8, pair[color], away, at, n)
            add(color, home, 8, pair[color], home, at, n)
            reduce_send(color, 0, p)
            if p == 2 and color == 1 and not state_ready:
                state_ready = True
                state_to_cover()
        elif stage_no < 4:
            s = stage_no - 1
            size = 4 >> s
            wait_on(rec[color][s].at[:, pl.ds(at, n)], rs_recv.at[color, s, p])
            first = base(color, stage_no)
            bit = bits[color][stage_no]
            add(color, first + (1 - bit) * size, size, rec[color][s], (1 - bit) * size, at, n)
            add(color, first + bit * size, size, rec[color][s], bit * size, at, n)
            reduce_send(color, stage_no, p)
        elif stage_no == 4:
            wait_on(rec[color][3].at[:, pl.ds(at, n)], rs_recv.at[color, 3, p])
            slot = base(color, 4)
            add(color, slot, 1, rec[color][3], 0, at, n)
            adam(color, p)
            src = own[color].at[pl.ds(at, n)]
            dst = gat[color].at[c, slot, pl.ds(at, n)]
            pltpu.make_async_remote_copy(src, dst, ag_send.at[color, 0], ag_recv.at[color, 0, p], device_id=to_z1, device_id_type=MESH).start()
            pltpu.make_async_copy(src, dst, loc_sem.at[color, p]).start()
            pltpu.make_async_remote_copy(src, dst, dag_send.at[color], dag_recv.at[color], device_id=to_pair, device_id_type=MESH).start()
        else:
            s = stage_no - 5
            level = 4 - s
            size = 1 << s
            bit = bits[color][level - 1]
            arrived = base(color, level - 1) + (1 - bit) * size
            wait_on(gat[color].at[c, pl.ds(arrived, size), pl.ds(at, n)], ag_recv.at[color, s, p])
            if s == 0:
                wait_on(gat[color].at[c, base(color, 4), pl.ds(at, n)], loc_sem.at[color, p])
            if s < 3:
                block = gat[color].at[c, pl.ds(base(color, level - 1), 2 * size), pl.ds(at, n)]
                pltpu.make_async_remote_copy(block, block, ag_send.at[color, s + 1], ag_recv.at[color, s + 1, p], device_id=routes[color][level - 2], device_id_type=MESH).start()
            pair_out(color, arrived, size, p)
        if stage_no == 4:
            waited.add((color, p, 4))
            if sum(len(w) == 3 for w in waited) == 2 * len(PIECE):
                cover_to_state()
                for i, dst in enumerate((m_out, v_out, w_out)):
                    pltpu.make_async_copy(stage.at[i, pl.ds(MARGIN, SLICE_ROWS)], dst, state_sem.at[i]).start()

    for i, dst in enumerate((m_out, v_out, w_out)):
        wait_on(dst, state_sem.at[i])
    for color in (0, 1):
        wait_on(gat[color].at[1 - c], dag_recv.at[color])
        wait_on(gat[color].at[c], dag_send.at[color])
        wait_on(acc[color], pr_send.at[color])
        for s in range(4):
            wait_on(rec[color][s], rs_send.at[color, s])
        wait_on(own[color], ag_send.at[color, 0])
        for s in range(1, 4):
            wait_on(gat[color].at[0, pl.ds(0, 1 << s)], ag_send.at[color, s])


def place_kernel(in_a, in_b, e_out, a_out, f1_out, f2_out, b_out, buf_a, buf_b, in_sem, out_sem):
    outs = (e_out, a_out, f1_out, f2_out, b_out)
    ins, buf = (in_a, in_b), (buf_a, buf_b)
    places = [(color, d) for d in range(NDEV) for color in (0, 1)]
    for color, d in places:
        slot = slot_of(color, d // 2)
        pltpu.make_async_copy(ins[color].at[d % 2, slot], buf[color].at[d], in_sem.at[color, d]).start()
    row = lax.broadcasted_iota(jnp.int32, (32, 128), 0)
    lane = lax.broadcasted_iota(jnp.int32, (32, 128), 1)
    tile_order = (row % 8) * 4 + row // 8
    started = []
    for d in range(NDEV):
        for color in (0, 1):
            pltpu.make_async_copy(ins[color].at[d % 2, slot_of(color, d // 2)], buf[color].at[d], in_sem.at[color, d]).wait()
        first = merge_row(d)
        last = merge_row(d + 1) if d + 1 < NDEV else STARTS[-1]
        if d > 0:
            mine = first - start_row(d)
            his = first - start_row(d - 1) - HALF
            flat = tile_order if PERM_LO <= first < PERM_HI else row
            keep = 2 * flat + lane // 64 >= 3597 * d - 2 * first
            new = buf_a[d, pl.ds(mine, 32), :].astype(jnp.float32)
            old = buf_b[d - 1, pl.ds(his, 32), :].astype(jnp.float32)
            buf_a[d, pl.ds(mine, 32), :] = jnp.where(keep, new, old).astype(jnp.bfloat16)
        for color in (0, 1):
            lo = max(first, start_row(d) + color * HALF)
            hi = min(last, start_row(d) + (color + 1) * HALF)
            for tensor, at, off, n in segments(lo, hi - lo):
                copy = pltpu.make_async_copy(buf[color].at[d, pl.ds(lo + off - start_row(d) - color * HALF, n)], outs[tensor].at[pl.ds(at, n)], out_sem.at[len(started)])
                copy.start()
                started.append(copy)
    for copy in started:
        copy.wait()


def tile_rows(tensor):
    return tensor.reshape(-1, 8, 4, 128).transpose(0, 2, 1, 3).reshape(-1, 128)


def untile(rows, shape):
    return rows.reshape(-1, 4, 8, 128).transpose(0, 2, 1, 3).reshape(shape)


def solution(mesh):
    def local_step(g_embed, g_attn, g_ffn_in, g_ffn_out, g_vec, m_shard, v_shard, w_shard):
        grads = (g_embed[0], tile_rows(g_attn[0]), tile_rows(g_ffn_in[0]), g_ffn_out[0].reshape(-1, 128), g_vec[0].reshape(-1, 128))
        state = [jnp.pad(s, (0, PAD)).reshape(SLICE_ROWS, 128) for s in (m_shard, v_shard, w_shard)]
        any_spec = pl.BlockSpec(memory_space=pl.ANY)
        f32, bf16 = jnp.float32, jnp.bfloat16
        np_ = len(PIECE)
        gathered = jax.ShapeDtypeStruct((2, 16, HALF, 128), bf16)
        flat = jax.ShapeDtypeStruct((SLICE_ROWS, 128), f32)
        both = lambda *shape: [pltpu.VMEM(shape, f32)] * 2
        dma = pltpu.SemaphoreType.DMA
        out_a, out_b, m_new, v_new, w_new = pl.pallas_call(
            big_kernel,
            out_shape=(gathered, gathered, flat, flat, flat),
            in_specs=[any_spec] * 8,
            out_specs=[any_spec] * 5,
            scratch_shapes=both(16, HALF, 128) + both(16, HALF, 128) + both(8, HALF, 128) + both(4, HALF, 128) + both(2, HALF, 128) + both(1, HALF, 128)
            + [pltpu.VMEM((HALF, 128), bf16)] * 2
            + [pltpu.VMEM((3, SLICE_ROWS + 2 * MARGIN, 128), f32), pltpu.VMEM((3, COVER, 128), f32)]
            + [dma((2, len(LOAD))), dma((2, len(LOAD))), dma((2,)), dma((2, 4, np_)), dma((2, 4)), dma((2, 4, np_)), dma((2, 4)), dma((2, np_)), dma((2,)), dma((2,)), dma((3,))],
            compiler_params=pltpu.CompilerParams(collective_id=0, has_side_effects=True, vmem_limit_bytes=62 * 1024 * 1024),
            name='reduce_adam_gather',
        )(*grads, *state)
        placed = pl.pallas_call(
            place_kernel,
            out_shape=[jax.ShapeDtypeStruct((n, 128), bf16) for n in TENSOR_ROWS],
            in_specs=[any_spec] * 2,
            out_specs=[any_spec] * 5,
            scratch_shapes=[pltpu.VMEM((NDEV, HALF, 128), bf16)] * 2 + [dma((2, NDEV)), dma((2 * NDEV + 8,))],
            compiler_params=pltpu.CompilerParams(vmem_limit_bytes=40 * 1024 * 1024),
            name='place',
        )(out_a, out_b)
        e, a, f1, f2, b = placed
        tensors = (e, untile(a, (16, 128, 512)), untile(f1, (16, 128, 512)), f2.reshape(16, 512, 128), b.reshape(16, 1664))
        chip = ((lax.axis_index('outer') * 2 + lax.axis_index('middle')) * 4 + lax.axis_index('inner')) // 2
        blocks = [lax.dynamic_slice_in_dim(e, chip * 2048, 2048, axis=0)]
        for t in (a, f1):
            rows = lax.dynamic_slice_in_dim(t.reshape(16, 16, 32, 128), chip, 1, axis=1)
            blocks.append(untile(rows, (512, 128)))
        blocks.append(lax.dynamic_slice_in_dim(f2.reshape(16, 512, 128), chip * 32, 32, axis=1).reshape(512, 128))
        blocks.append(lax.dynamic_slice_in_dim(tensors[4], chip * 104, 104, axis=1).reshape(13, 128))
        wide = jnp.concatenate([t.astype(f32) for t in blocks], axis=0)
        w_chip = lax.optimization_barrier(wide).reshape(1, -1).astype(bf16)
        state = tuple(s.reshape(-1)[:SLICE] for s in (m_new, v_new, w_new))
        return state + tensors + (w_chip,)

    return jax.shard_map(local_step, mesh=mesh, in_specs=(P(MESH_AXES),) * 8, out_specs=(P(MESH_AXES),) * 3 + (P(),) * 5 + (P(MESH_AXES),), check_vma=False)
```

time: 796 us -> 262 us (0.33)
  waiting for transfers between devices: 702 us -> 0 us
  Pallas kernels: 0 us -> 227 us
  local copies, waits for them, and re-layouts: 74.8 us -> 33.3 us
  between operations: 14.2 us -> 0.8 us
    unnamed x4 -> x0, waiting for transfers between devices: 702 us -> none
    pallas_call x0 -> x2, Pallas kernels: none -> 227 us  [the longest x1 211 us: local_step(): pl.pallas_call(big_kernel, out_shape=(gathered, gathered, flat, flat, fla...]
    unnamed x33 -> x16, local copies, waits for them, and re-layouts: 45.1 us -> 23.6 us
    broadcast_in_dim x1 -> x0, local copies, waits for them, and re-layouts: 11.3 us -> none  [own_chip_block(): return jnp.concatenate(block_list)[None, :]]
    slice x4 -> x0, local copies, waits for them, and re-layouts: 9.52 us -> none  [split_tensors(): pieces.append(flat_values[offset:offset + count].reshape(shape))]
  transfers between devices with their start and end apart: 2 -> 0, of which waited for: 2 -> 0; matrix products, arithmetic and copies ran while one was open for 0% -> 0% of each run, Pallas kernels for 0% -> 0%
where the time goes in v1:
time: 262 us
  Pallas kernels  227 us (87%)
  local copies, waits for them, and re-layouts  33.3 us (13%)
    pallas_call x1, Pallas kernels, local_step(): pl.pallas_call(big_kernel, out_shape=(gathered, gathered, flat, flat, fla...  211 us
    unnamed x16, local copies, waits for them, and re-layouts  23.6 us
    pallas_call x1, Pallas kernels, local_step(): pl.pallas_call(place_kernel, out_shape=[jax.ShapeDtypeStruct((n, 128), bf...  16.2 us

profile of v1, /device:TPU:0, one launch (start us, length us, event | category | flops | bytes accessed | tf_op | source)
XLA Modules:
  0.0 261.6 jit_solution(18061422529954662530)
XLA Ops:
  0.6 1.5 reshape_squeeze.15.gb
  2.2 2.2 pad_bitcast_fusion.2.m_in
  4.4 2.8 %pad_bitcast_fusion = (f32[1800,128]{1,0:T(8,128)}, f32[1800,128]{1,0:T(8,128)}) fusion(f32[230208]{0:T(1024)} %param.15, f32[230208]{0:T(1024)} %param.14), kind=kLoop, calls=%fused_computation.2 | loop fusion | bytes 3684864 | tf_op jit(solution)/shard_map/reshape | solution.py:371
  7.2 211.3 %reduce_adam_gather.1 = (bf16[2,16,928,128]{3,2,1,0:T(8,128)(2,1)}, bf16[2,16,928,128]{3,2,1,0:T(8,128)(2,1)}, f32[1800,128]{1,0:T(8,128)}, f32[1800,128]{1,0:T(8,128)}, f32[1800,128]{1,0:T(8,128)}) custom-call(f32[32768,128]{1,0:T(8,128)} %bitcast.59, f32[8192,128]{1,0:T(8,128)} %bitcast.60, f32[8192,128]{1,0:T(8,128)} %bitcast.61, f32[8192,128]{1,0:T(8,128)} %bitcast.62, ...), custom_call_target="tpu_custom_call" | custom-call | tf_op jit(solution)/shard_map/reduce_adam_gather/pallas_call | solution.py:379
  218.5 0.0 copy-start
  218.5 3.1 %copy-done = bf16[2,16,928,128]{3,2,1,0:T(8,128)(2,1)S(1)} copy-done((bf16[2,16,928,128]{3,2,1,0:T(8,128)(2,1)S(1)}, bf16[2,16,928,128]{3,2,1,0:T(8,128)(2,1)}, u32[]{:S(2)}) %copy-start) | copy-done | bytes 7602200
  221.6 16.2 %place.1 = (bf16[32768,128]{1,0:T(8,128)(2,1)}, bf16[8192,128]{1,0:T(8,128)(2,1)}, bf16[8192,128]{1,0:T(8,128)(2,1)}, bf16[8192,128]{1,0:T(8,128)(2,1)}, bf16[208,128]{1,0:T(8,128)(2,1)S(1)}) custom-call(bf16[2,16,928,128]{3,2,1,0:T(8,128)(2,1)S(1)} %copy-done, bf16[2,16,928,128]{3,2,1,0:T(8,128)(2,1)} %get-tuple-element.23.in_b), custom_call_target="tpu_custom_call" | custom-call | tf_op jit(solution)/shard_map/place/pallas_call | solution.py:391
  237.8 0.0 copy-start.2
  237.8 0.1 reshape.112
  237.9 0.0 copy-start.3
  237.9 1.2 dynamic-slice_dynamic-update-slice_fusion
  239.1 0.9 dynamic-slice_bitcast_fusion.1
  240.1 0.0 copy-start.1
  240.1 0.1 copy.18
  240.2 1.0 dynamic-slice_bitcast_fusion
  241.1 0.1 copy.20
  241.2 0.9 constant_dynamic-slice_fusion.1
  242.2 0.1 constant_dynamic-slice_fusion
  242.3 0.1 convert_element_type.54
  242.4 15.1 %copy.25 = bf16[1,1,3597,128]{3,1,2,0:T(2,128)(2,1)} copy(bf16[1,1,3597,128]{3,2,1,0:T(8,128)(2,1)S(1)} %bitcast.63) | data formatting | bytes 1841664
  257.5 2.2 copy.33
  259.6 0.0 copy-done.2
  259.6 1.0 copy.34
  260.6 0.0 copy-done.3
  260.6 0.0 copy-done.1
  260.6 1.0 copy.35
  (4 shorter events, 0.1 us)
Async XLA Ops:
  218.5 3.2 %copy-start = (bf16[2,16,928,128]{3,2,1,0:T(8,128)(2,1)S(1)}, bf16[2,16,928,128]{3,2,1,0:T(8,128)(2,1)}, u32[]{:S(2)}) copy-start(bf16[2,16,928,128]{3,2,1,0:T(8,128)(2,1)} %get-tuple-element.22.in_a) | copy-start | bytes 22806532
  237.8 21.8 %copy-start.2 = (f32[1800,128]{1,0:T(8,128)S(1)}, f32[1800,128]{1,0:T(8,128)}, u32[]{:S(2)}) copy-start(f32[1800,128]{1,0:T(8,128)} %get-tuple-element.20) | copy-start | bytes 2764804
  237.9 22.7 %copy-start.3 = (bf16[16,1664]{1,0:T(8,128)(2,1)}, bf16[16,1664]{1,0:T(8,128)(2,1)S(1)}, u32[]{:S(2)}) copy-start(bf16[16,1664]{1,0:T(8,128)(2,1)S(1)} %reshape.112) | copy-start | bytes 159748
  240.1 20.6 %copy-start.1 = (f32[1800,128]{1,0:T(8,128)S(1)}, f32[1800,128]{1,0:T(8,128)}, u32[]{:S(2)}) copy-start(f32[1800,128]{1,0:T(8,128)} %get-tuple-element.21) | copy-start | bytes 2764804

commit v2 on v1

v2 whole, which is shorter than its diff:
```python
import functools

import jax
import jax.numpy as jnp
from jax import lax
from jax.experimental import pallas as pl
from jax.experimental.pallas import tpu as pltpu
from jax.sharding import PartitionSpec as P

MESH_AXES = ('outer', 'middle', 'inner')
MESH = pl.DeviceIdType.MESH
BETA1, BETA2, EPS, RATE, STEP = 0.9, 0.98, 1e-9, 0.05, 3

NDEV = 32
GROUP = 32
LANES = 128
TILE = 8
BLOCK = 1024
LAST = NDEV - 1
LAST_START = 55696
SPAN = 3597
COLORS = (0, 1)
REST = 1792
ROWS = 1856
HALF = ROWS // 2
SLICE = 230208
SLICE_ROWS = 1800
MARGIN = 64
VMEM = 62 << 20
COVER = ROWS + 8
TENSOR_ROWS = (32768, 8192, 8192, 8192, 208)
STARTS = (0, 32768, 40960, 49152, 57344, 57552)
PERM_LO, PERM_HI = 32768, 49152
PIECES = (32, 64) + (128,) * 6 + (64,)
LOADS = (32, 64, 128, 256, 448)
E_SLOTS = 9


def bounds(sizes):
    out, at = [], 0
    for n in sizes:
        out.append((at, n))
        at += n
    return out


PIECE = bounds(PIECES)
LOAD = bounds(LOADS)
LOAD_OF = [next(i for i, (a, n) in enumerate(LOAD) if a <= p < a + n) for p, _ in PIECE]
LOAD_MODEL = (2, 0.0136, 3, 40, 0.25)
LINK_RATE = 46600


def start_row(d):
    return LAST_START if d == LAST else 32 * (SPAN * d // 64)


def merge_row(d):
    return 32 * (SPAN * d // 64)


def segments(row, n):
    out = []
    for t in range(5):
        lo, hi = max(row, STARTS[t]), min(row + n, STARTS[t + 1])
        if lo < hi:
            out.append((t, lo - STARTS[t], lo - row, hi - lo))
    return out


def slot_of(color, k):
    x, y, z0, z1 = k % 2, k // 2 % 2, k // 4 % 2, k // 8
    return (x * 8 + z0 * 4 + y * 2 + z1) if color == 0 else (y * 8 + z0 * 4 + x * 2 + z1)


def event_order():
    loaded, rate, hop, ahead, step = LOAD_MODEL
    ready = []
    for at, n in LOAD:
        for color in COLORS:
            loaded += n * rate
        ready.append(loaded)
    waiting = [(ready[LOAD_OF[p]], 0, p, color) for p in range(len(PIECE)) for color in COLORS]
    free = dict.fromkeys('xyz', 0)
    names = ('xzyz', 'yzxz')
    now, events = 0, []
    while waiting:
        def begin(e):
            return max(now, e[0], 0 if e[1] else free[names[e[3]][0]] - ahead)

        at = min(map(begin, waiting))
        time, stage, p, color = e = max((e for e in waiting if begin(e) <= at), key=lambda e: (e[1], -e[2], -e[3]))
        waiting.remove(e)
        events.append(e[1:])
        now = at + step * (1 if stage else 3)
        if stage < 8:
            link = names[color][min(stage, 7 - stage)]
            rows = PIECE[p][1] * (8 >> stage if stage < 4 else (1 << stage) / GROUP)
            free[link] = max(now, free[link]) + rows * LANES * 4 / LINK_RATE
            waiting.append((free[link] + hop, stage + 1, p, color))
    return events


def big_kernel(ge, ga, gf1, gf2, gb, m_in, v_in, w_in, out_a, out_b, m_out, v_out, w_out, acc_a, acc_b, pair_a, pair_b, r1_a, r1_b, r2_a, r2_b, r3_a, r3_b, r4_a, r4_b, own_a, own_b, line_m, line_v, line_w, stage, cov, ld_sem, pr_recv, pr_send, rs_recv, rs_send, ag_recv, ag_send, loc_sem, dag_recv, dag_send, state_sem):
    grads = (ge, ga, gf1, gf2, gb)
    acc, pair, own, gat = (acc_a, acc_b), (pair_a, pair_b), (own_a, own_b), (out_a, out_b)
    rec = ((r1_a, r2_a, r3_a, r4_a), (r1_b, r2_b, r3_b, r4_b))
    z, y, inner = lax.axis_index('outer'), lax.axis_index('middle'), lax.axis_index('inner')
    x, c = inner // 2, inner % 2
    z0, z1 = z % 2, z // 2
    dev = (z * 2 + y) * 4 + inner
    to_pair = {'inner': inner + 1 - 2 * c}
    to_x = {'inner': inner + 2 - 4 * x}
    to_y = {'middle': 1 - y}
    to_z0 = {'outer': z + 1 - 2 * z0}
    to_z1 = {'outer': z + 2 - 4 * z1}
    routes = ((to_x, to_z0, to_y, to_z1), (to_y, to_z0, to_x, to_z1))
    bits = ((x, z0, y, z1), (y, z0, x, z1))

    barrier = pltpu.get_barrier_semaphore()
    for to in (to_pair, to_x, to_y, to_z0, to_z1):
        pl.semaphore_signal(barrier, inc=1, device_id=to, device_id_type=MESH)

    lines = (line_m, line_v, line_w)
    state_in = [pltpu.make_async_copy(src, lines[i], state_sem.at[i]) for i, src in enumerate((m_in, v_in, w_in))]
    for copy in state_in:
        copy.start()
    pl.semaphore_wait(barrier, 5)

    def load_one(color, i, tensor, row, slot, at, n, mine):
        src = grads[tensor].at[pl.ds(row, n)]
        if mine:
            pltpu.make_async_copy(src, acc[color].at[slot, pl.ds(at, n)], ld_sem.at[color, i]).start()
        else:
            pltpu.make_async_remote_copy(src, pair[color].at[slot, pl.ds(at, n)], pr_send.at[color], pr_recv.at[color, i], device_id=to_pair, device_id_type=MESH).start()

    def load(i):
        at, n = LOAD[i]
        for color in COLORS:
            @pl.loop(0, E_SLOTS)
            def _(k):
                slot = slot_of(color, k)
                for mine in (False, True):
                    d = 2 * k + (c if mine else 1 - c)
                    row = pl.multiple_of(GROUP * ((SPAN * d) // 64), GROUP) + color * HALF + at
                    load_one(color, i, 0, row, slot, at, n, mine)
            for core in COLORS:
                @pl.when(c == core)
                def _():
                    for k in range(E_SLOTS, NDEV // 2):
                        slot = slot_of(color, k)
                        for mine in (False, True):
                            d = 2 * k + (core if mine else 1 - core)
                            for tensor, row, off, rows in segments(start_row(d) + color * HALF + at, n):
                                load_one(color, i, tensor, row, slot, at + off, rows, mine)

    def wait_on(ref, sem):
        pltpu.make_async_copy(ref, ref, sem).wait()

    def add(color, into, slots, src, first, at, n):
        @pl.loop(0, slots)
        def _(i):
            acc[color][into + i, pl.ds(at, n), :] += src[first + i, pl.ds(at, n), :]

    def base(color, level):
        return sum((bits[color][i] * (TILE >> i) for i in range(level)), 0 * c)

    def reduce_send(color, s, p):
        at, n = PIECE[p]
        size = TILE >> s
        first = base(color, s) + (1 - bits[color][s]) * size
        pltpu.make_async_remote_copy(acc[color].at[pl.ds(first, size), pl.ds(at, n)], rec[color][s].at[:, pl.ds(at, n)], rs_send.at[color, s], rs_recv.at[color, s, p], device_id=routes[color][s], device_id_type=MESH).start()

    def pair_out(color, slot, size, p):
        at, n = PIECE[p]
        block = gat[color].at[c, pl.ds(slot, size), pl.ds(at, n)]
        pltpu.make_async_remote_copy(block, block, dag_send.at[color], dag_recv.at[color], device_id=to_pair, device_id_type=MESH).start()

    def adam_block(g, load_state, store_state):
        g = g * (1.0 / NDEV)
        m = BETA1 * load_state(0) + (1.0 - BETA1) * g
        v = BETA2 * load_state(1) + (1.0 - BETA2) * (g * g)
        m_hat = m / (1.0 - BETA1 ** STEP)
        v_hat = v / (1.0 - BETA2 ** STEP)
        w = load_state(2) - RATE * m_hat / (jnp.sqrt(v_hat) + EPS)
        store_state(0, m)
        store_state(1, v)
        store_state(2, w)
        return w

    cover_start = jnp.where(dev == LAST, LAST_START, GROUP * ((SPAN * dev) // 64))

    def adam(color, p):
        at, n = PIECE[p]
        slot = base(color, 4)

        @pl.loop(0, n // GROUP)
        def _(j):
            r = pl.multiple_of(at + j * GROUP, GROUP)
            f = pl.multiple_of(color * HALF + r, GROUP)
            row = cover_start + f
            permuted = (row >= PERM_LO) & (row < PERM_HI)

            def group(index):
                for t in range(2):
                    parts = []
                    for q in (2 * t, 2 * t + 1):
                        where = index(f, q)

                        def keep(i, value, where=where):
                            cov[i, where, :] = value

                        parts.append(adam_block(acc[color][slot, pl.ds(r + TILE * q, TILE), :], lambda i, where=where: cov[i, where, :], keep))
                    own[color][pl.ds(r + 16 * t, 16), :] = jnp.concatenate(parts, axis=0).astype(jnp.bfloat16)

            @pl.when(permuted)
            def _():
                group(lambda f, q: pl.ds(f + q, TILE, stride=4))

            @pl.when(jnp.logical_not(permuted))
            def _():
                group(lambda f, q: pl.ds(f + TILE * q, TILE))

    half_rows = jnp.where(dev == LAST, 115, (SPAN * dev) % 64)
    shift = half_rows // 2
    lane = lax.broadcasted_iota(jnp.int32, (GROUP, LANES), 1)

    def moved(first, second):
        return jnp.where(lane < 64, pltpu.roll(first, 64, 1), pltpu.roll(second, 64, 1))

    def state_rows():
        for i, copy in enumerate(state_in):
            copy.wait()
            stage[i, 0:MARGIN, :] = jnp.zeros((MARGIN, LANES), jnp.float32)
            stage[i, MARGIN + SLICE_ROWS - TILE:, :] = jnp.zeros((MARGIN + TILE, LANES), jnp.float32)
            cov[i, ROWS:, :] = jnp.zeros((COVER - ROWS, LANES), jnp.float32)
            for r in range(REST, 1798):
                stage[i, MARGIN + r:MARGIN + r + 1, :] = lines[i][LANES * r:LANES * r + LANES].reshape(1, LANES)
            stage[i, MARGIN + 1798:MARGIN + 1799, 0:64] = lines[i][SLICE - 64:].reshape(1, 64)

    def state_rows_part(t):
        @pl.loop(GROUP * t, GROUP * t + GROUP)
        def _(j):
            for i in range(3):
                stage[i, pl.ds(pl.multiple_of(MARGIN + j * TILE, TILE), TILE), :] = lines[i][pl.ds(pl.multiple_of(j * BLOCK, BLOCK), BLOCK)].reshape(TILE, LANES)

    def state_to_cover(t):
        @pl.loop(6 * t, min(6 * t + 6, ROWS // GROUP))
        def _(j):
            f = pl.multiple_of(j * GROUP, GROUP)
            r = MARGIN + f - shift
            for i in range(3):
                here = stage[i, pl.ds(r, GROUP), :]
                before = stage[i, pl.ds(r - 1, GROUP), :]
                cov[i, pl.ds(f, GROUP), :] = jnp.where(c == 1, moved(before, here), here)

    def cover_to_state(t):
        @pl.loop(15 * t, 15 * t + 15)
        def _(j):
            r = pl.multiple_of(j * TILE, TILE)
            for i in range(3):
                here = cov[i, pl.ds(r + shift, TILE), :]
                after = cov[i, pl.ds(r + shift + 1, TILE), :]
                both = jnp.where(lane[:TILE] < 64, pltpu.roll(here, 64, 1), pltpu.roll(after, 64, 1))
                stage[i, pl.ds(pl.multiple_of(MARGIN + r, TILE), TILE), :] = jnp.where(c == 1, both, here)

    def state_out():
        for i, dst in enumerate((m_out, v_out, w_out)):
            pltpu.make_async_copy(stage.at[i, pl.ds(MARGIN, SLICE_ROWS)], dst, state_sem.at[i]).start()

    before_adam = [state_rows] + [functools.partial(state_rows_part, t) for t in range(7)] + [functools.partial(state_to_cover, t) for t in range(10)]
    after_adam = [functools.partial(cover_to_state, t) for t in range(15)] + [state_out]
    adams_left = 2 * len(PIECE)
    load(0)
    load(1)
    events = event_order()
    loads_started = 2
    waited = set()
    for place, (stage_no, p, color) in enumerate(events):
        at, n = PIECE[p]
        if stage_no == 0:
            i = LOAD_OF[p]
            while loads_started < min(i + 2, len(LOAD)):
                load(loads_started)
                loads_started += 1
            if (color, i) not in waited:
                waited.add((color, i))
                la, ln = LOAD[i]
                wait_on(acc[color].at[:, pl.ds(la, ln)], ld_sem.at[color, i])
                wait_on(pair[color].at[:, pl.ds(la, ln)], pr_recv.at[color, i])
            away, home = (1 - bits[color][0]) * TILE, bits[color][0] * TILE
            add(color, away, TILE, pair[color], away, at, n)
            add(color, home, TILE, pair[color], home, at, n)
            reduce_send(color, 0, p)
        elif stage_no < 4:
            s = stage_no - 1
            size = 4 >> s
            wait_on(rec[color][s].at[:, pl.ds(at, n)], rs_recv.at[color, s, p])
            first = base(color, stage_no)
            bit = bits[color][stage_no]
            add(color, first + (1 - bit) * size, size, rec[color][s], (1 - bit) * size, at, n)
            add(color, first + bit * size, size, rec[color][s], bit * size, at, n)
            reduce_send(color, stage_no, p)
        elif stage_no == 4:
            while before_adam:
                before_adam.pop(0)()
            adams_left -= 1
            wait_on(rec[color][3].at[:, pl.ds(at, n)], rs_recv.at[color, 3, p])
            slot = base(color, 4)
            add(color, slot, 1, rec[color][3], 0, at, n)
            adam(color, p)
            src = own[color].at[pl.ds(at, n)]
            dst = gat[color].at[c, slot, pl.ds(at, n)]
            pltpu.make_async_remote_copy(src, dst, ag_send.at[color, 0], ag_recv.at[color, 0, p], device_id=to_z1, device_id_type=MESH).start()
            pltpu.make_async_copy(src, dst, loc_sem.at[color, p]).start()
            pltpu.make_async_remote_copy(src, dst, dag_send.at[color], dag_recv.at[color], device_id=to_pair, device_id_type=MESH).start()
        else:
            s = stage_no - 5
            level = 4 - s
            size = 1 << s
            bit = bits[color][level - 1]
            arrived = base(color, level - 1) + (1 - bit) * size
            wait_on(gat[color].at[c, pl.ds(arrived, size), pl.ds(at, n)], ag_recv.at[color, s, p])
            if s == 0:
                wait_on(gat[color].at[c, base(color, 4), pl.ds(at, n)], loc_sem.at[color, p])
            if s < 3:
                block = gat[color].at[c, pl.ds(base(color, level - 1), 2 * size), pl.ds(at, n)]
                pltpu.make_async_remote_copy(block, block, ag_send.at[color, s + 1], ag_recv.at[color, s + 1, p], device_id=routes[color][level - 2], device_id_type=MESH).start()
            pair_out(color, arrived, size, p)
        if place >= 4 and before_adam:
            before_adam.pop(0)()
        if adams_left == 0 and after_adam:
            after_adam.pop(0)()
    for job in after_adam:
        job()

    for i, dst in enumerate((m_out, v_out, w_out)):
        wait_on(dst, state_sem.at[i])
    for color in COLORS:
        wait_on(gat[color].at[1 - c], dag_recv.at[color])
        wait_on(gat[color].at[c], dag_send.at[color])
        wait_on(acc[color], pr_send.at[color])
        for s in range(4):
            wait_on(rec[color][s], rs_send.at[color, s])
        wait_on(own[color], ag_send.at[color, 0])
        for s in range(1, 4):
            wait_on(gat[color].at[0, pl.ds(0, 1 << s)], ag_send.at[color, s])


def place_kernel(in_a, in_b, m_in, v_in, w_in, e_out, a_out, f1_out, f2_out, b_out, m_out, v_out, w_out, chip_out, buf, state, loose, vec, tail, block, in_sem, out_sem, state_sem, chip_sem):
    outs = (e_out, a_out, f1_out, f2_out, b_out)
    ins = (in_a, in_b)
    chip = (lax.axis_index('outer') * 2 + lax.axis_index('middle')) * 2 + lax.axis_index('inner') // 2

    def arriving(color, d):
        return pltpu.make_async_copy(ins[color].at[d % 2, slot_of(color, d // 2)], buf.at[d, pl.ds(color * HALF, HALF)], in_sem.at[color, d])

    for d in range(NDEV):
        for color in COLORS:
            arriving(color, d).start()
    kept = [(pltpu.make_async_copy(src, state.at[i], state_sem.at[i]), pltpu.make_async_copy(state.at[i], dst, state_sem.at[i])) for i, (src, dst) in enumerate(((m_in, m_out), (v_in, v_out), (w_in, w_out)))]
    for first, _ in kept:
        first.start()
    row = lax.broadcasted_iota(jnp.int32, (GROUP, LANES), 0)
    lane = lax.broadcasted_iota(jnp.int32, (GROUP, LANES), 1)
    tile_order = (row % TILE) * 4 + row // TILE
    started = []
    for d in range(NDEV):
        for color in COLORS:
            arriving(color, d).wait()
        first = merge_row(d)
        last = merge_row(d + 1) if d + 1 < NDEV else STARTS[-1]
        mine = first - start_row(d)
        if d > 0:
            his = first - start_row(d - 1)
            flat = tile_order if PERM_LO <= first < PERM_HI else row
            keep = 2 * flat + lane // 64 >= SPAN * d - 2 * first
            new = buf[d, mine:mine + GROUP, :].astype(jnp.float32)
            old = buf[d - 1, his:his + GROUP, :].astype(jnp.float32)
            buf[d, mine:mine + GROUP, :] = jnp.where(keep, new, old).astype(jnp.bfloat16)
        for tensor, at, off, n in segments(first, last - first):
            copy = pltpu.make_async_copy(buf.at[d, pl.ds(mine + off, n)], outs[tensor].at[pl.ds(at, n)], out_sem.at[len(started)])
            copy.start()
            started.append(copy)
    for first, second in kept:
        first.wait()
        second.start()

    def rows_of(group):
        d = (64 * group + 63) // SPAN
        begin = jnp.where(d == LAST, LAST_START, GROUP * ((SPAN * d) // 64))
        return buf[d, pl.ds(pl.multiple_of(GROUP * group - begin, 16), GROUP), :].astype(jnp.float32)

    def put(at, rows):
        block[0:1, pl.ds(pl.multiple_of(at * LANES, BLOCK), BLOCK)] = rows.reshape(1, BLOCK).astype(jnp.bfloat16)

    @pl.loop(0, 64)
    def _(j):
        rows = rows_of(chip * 64 + j)
        for q in range(4):
            put(GROUP * j + TILE * q, rows[TILE * q:TILE * q + TILE])

    @pl.loop(0, 16)
    def _(layer):
        for t in (1, 2):
            rows = rows_of(STARTS[t] // GROUP + layer * 16 + chip)
            for q in range(4):
                loose[t - 1, pl.ds(q, TILE, stride=4), :] = rows[TILE * q:TILE * q + TILE]
            for q in range(4):
                put(1536 + 512 * t + GROUP * layer + TILE * q, loose[t - 1, TILE * q:TILE * q + TILE, :])
        rows = rows_of(STARTS[3] // GROUP + layer * 16 + chip)
        for q in range(4):
            put(3072 + GROUP * layer + TILE * q, rows[TILE * q:TILE * q + TILE])

    at = STARTS[4] - start_row(LAST)
    vec[0:208, :] = buf[LAST, at:at + 208, :].astype(jnp.float32)
    vec[208:, :] = jnp.zeros((16, LANES), jnp.float32)
    tail[...] = jnp.zeros_like(tail)
    begin = (104 * chip) % LANES
    line = lax.broadcasted_iota(jnp.int32, (TILE, LANES), 1)
    for layer in range(16):
        source = layer * 13 + (104 * chip) // LANES
        to = layer * 104 // LANES
        off = layer * 104 % LANES
        turn = (off - begin + LANES) % LANES
        one = pltpu.roll(vec[pl.ds(source, TILE), :], turn, 1)
        two = pltpu.roll(vec[pl.ds(source + 1, TILE), :], turn, 1)
        t = (line - off + LANES) % LANES
        got = jnp.where(begin + t < LANES, one, two)
        here = (t < 104) & (line >= off)
        tail[to:to + 1, :] = jnp.where(here, got, tail[pl.ds(to, TILE), :])[0:1]
        if off + 104 > LANES:
            there = (t < 104) & (line < off)
            tail[to + 1:to + 2, :] = jnp.where(there, got, tail[pl.ds(to + 1, TILE), :])[0:1]
    put(3584, tail[0:TILE, :])
    block[0:1, 3592 * LANES:] = tail[TILE:16, :].reshape(1, BLOCK)[:, 0:640].astype(jnp.bfloat16)
    send = pltpu.make_async_copy(block, chip_out, chip_sem)
    send.start()
    for copy in started:
        copy.wait()
    for _, second in kept:
        second.wait()
    send.wait()


def tile_rows(tensor):
    return tensor.reshape(-1, TILE, 4, LANES).transpose(0, 2, 1, 3).reshape(-1, LANES)


def untile(rows, shape):
    return rows.reshape(-1, 4, TILE, LANES).transpose(0, 2, 1, 3).reshape(shape)


def solution(mesh):
    def local_step(g_embed, g_attn, g_ffn_in, g_ffn_out, g_vec, m_shard, v_shard, w_shard):
        grads = (g_embed[0], tile_rows(g_attn[0]), tile_rows(g_ffn_in[0]), g_ffn_out[0].reshape(-1, LANES), g_vec[0].reshape(-1, LANES))
        state = (m_shard, v_shard, w_shard)
        any_spec = pl.BlockSpec(memory_space=pl.ANY)
        f32, bf16 = jnp.float32, jnp.bfloat16
        np_ = len(PIECE)
        gathered = jax.ShapeDtypeStruct((2, 16, HALF, LANES), bf16)
        flat = jax.ShapeDtypeStruct((SLICE_ROWS, LANES), f32)
        both = lambda *shape: [pltpu.VMEM(shape, f32)] * 2
        dma = pltpu.SemaphoreType.DMA
        out_a, out_b, m_new, v_new, w_new = pl.pallas_call(
            big_kernel,
            out_shape=(gathered, gathered, flat, flat, flat),
            in_specs=[any_spec] * TILE,
            out_specs=[any_spec] * 5,
            scratch_shapes=both(16, HALF, LANES) + both(16, HALF, LANES) + both(TILE, HALF, LANES) + both(4, HALF, LANES) + both(2, HALF, LANES) + both(1, HALF, LANES)
            + [pltpu.VMEM((HALF, LANES), bf16)] * 2
            + [pltpu.VMEM((SLICE,), f32)] * 3 + [pltpu.VMEM((3, SLICE_ROWS + 2 * MARGIN, LANES), f32), pltpu.VMEM((3, COVER, LANES), f32)]
            + [dma((2, len(LOAD))), dma((2, len(LOAD))), dma((2,)), dma((2, 4, np_)), dma((2, 4)), dma((2, 4, np_)), dma((2, 4)), dma((2, np_)), dma((2,)), dma((2,)), dma((3,))],
            compiler_params=pltpu.CompilerParams(collective_id=0, has_side_effects=True, vmem_limit_bytes=VMEM),
            name='reduce_adam_gather',
        )(*grads, *state)
        placed = pl.pallas_call(
            place_kernel,
            out_shape=[jax.ShapeDtypeStruct((n, LANES), bf16) for n in TENSOR_ROWS] + [flat] * 3 + [jax.ShapeDtypeStruct((1, 2 * SLICE), bf16)],
            in_specs=[any_spec] * 5,
            out_specs=[any_spec] * 9,
            scratch_shapes=[pltpu.VMEM((NDEV, ROWS, LANES), bf16), pltpu.VMEM((3, SLICE_ROWS, LANES), f32), pltpu.VMEM((2, GROUP, LANES), f32), pltpu.VMEM((224, LANES), f32), pltpu.VMEM((24, LANES), f32), pltpu.VMEM((1, 2 * SLICE), bf16)]
            + [dma((2, NDEV)), dma((2 * NDEV,)), dma((3,)), dma(())],
            compiler_params=pltpu.CompilerParams(vmem_limit_bytes=VMEM),
            name='place',
        )(out_a, out_b, m_new, v_new, w_new)
        e, a, f1, f2, b, *state, w_chip = placed
        tensors = (e, untile(a, (16, LANES, 512)), untile(f1, (16, LANES, 512)), f2.reshape(16, 512, LANES), b.reshape(16, 1664))
        return tuple(t.reshape(-1)[:SLICE] for t in state) + tensors + (w_chip,)

    return jax.shard_map(local_step, mesh=mesh, in_specs=(P(MESH_AXES),) * TILE, out_specs=(P(MESH_AXES),) * 3 + (P(),) * 5 + (P(MESH_AXES),), check_vma=False)
```

time: 262 us -> 225 us (0.86)
  local copies, waits for them, and re-layouts: 33.3 us -> 3.07 us
  Pallas kernels: 227 us -> 221 us
    unnamed x16 -> x0, local copies, waits for them, and re-layouts: 23.6 us -> none
    pallas_call x1, Pallas kernels: 211 us -> 203 us  [local_step(): pl.pallas_call(big_kernel, out_shape=(gathered, gathered, flat, flat, fla...]
    reshape x2 -> x0, local copies, waits for them, and re-layouts: 4.97 us -> none  [local_step(): jnp.pad(s, (0, PAD)).reshape(SLICE_ROWS, 128)]
where the time goes in v2:
time: 225 us
  Pallas kernels  221 us (98%)
  local copies, waits for them, and re-layouts  3.07 us (1%)
    pallas_call x1, Pallas kernels, local_step(): pl.pallas_call(big_kernel, out_shape=(gathered, gathered, flat, flat, fla...  203 us
    pallas_call x1, Pallas kernels, local_step(): pl.pallas_call(place_kernel, out_shape=[jax.ShapeDtypeStruct((n, LANES),...  17.9 us

profile of v2, /device:TPU:0, one launch (start us, length us, event | category | flops | bytes accessed | tf_op | source)
XLA Modules:
  0.0 224.7 jit_solution(14119830057111120129)
XLA Ops:
  0.6 1.5 reshape_squeeze.15.gb
  2.2 203.0 %reduce_adam_gather.1 = (bf16[2,16,928,128]{3,2,1,0:T(8,128)(2,1)}, bf16[2,16,928,128]{3,2,1,0:T(8,128)(2,1)}, f32[1800,128]{1,0:T(8,128)}, f32[1800,128]{1,0:T(8,128)}, f32[1800,128]{1,0:T(8,128)}) custom-call(f32[32768,128]{1,0:T(8,128)} %bitcast.29, f32[8192,128]{1,0:T(8,128)} %bitcast.30, f32[8192,128]{1,0:T(8,128)} %bitcast.31, f32[8192,128]{1,0:T(8,128)} %bitcast.32, ...), custom_call_target="tpu_custom_call" | custom-call | tf_op jit(solution)/shard_map/reduce_adam_gather/pallas_call | solution.py:465
  205.2 17.9 %place.1 = (bf16[32768,128]{1,0:T(8,128)(2,1)}, bf16[8192,128]{1,0:T(8,128)(2,1)}, bf16[8192,128]{1,0:T(8,128)(2,1)}, bf16[8192,128]{1,0:T(8,128)(2,1)}, bf16[20...) custom-call(bf16[2,16,928,128]{3,2,1,0:T(8,128)(2,1)} %get-tuple-ele, ...), custom_call_target="tpu_custom_call" | custom-call | tf_op jit(solution)/shard_map/place/pallas_call | solution.py:477
  223.2 1.5 reshape.61

commit v3 on v2

--- a/solution.py
+++ b/solution.py
@@ -31,7 +31,6 @@
 TENSOR_ROWS = (32768, 8192, 8192, 8192, 208)
 STARTS = (0, 32768, 40960, 49152, 57344, 57552)
 PERM_LO, PERM_HI = 32768, 49152
-PIECES = (32, 64) + (128,) * 6 + (64,)
 LOADS = (32, 64, 128, 256, 448)
 E_SLOTS = 9
 
@@ -44,11 +43,14 @@
     return out
 
 
-PIECE = bounds(PIECES)
 LOAD = bounds(LOADS)
-LOAD_OF = [next(i for i, (a, n) in enumerate(LOAD) if a <= p < a + n) for p, _ in PIECE]
-LOAD_MODEL = (2, 0.0136, 3, 40, 0.25)
-LINK_RATE = 46600
+PIECES = HALF // GROUP
+LAGS = ((0, 3, 6, 8, 12, 19, 32, 36, 53), (0, 3, 6, 10, 16, 20, 31, 35, 52))
+SEQUENCE = ((8, 0), (6, 0), (8, 1), (7, 0), (2, 0), (3, 1), (1, 0), (0, 0), (5, 1), (5, 0), (4, 1), (6, 1), (4, 0), (2, 1), (1, 1), (0, 1), (3, 0), (7, 1))
+STEPS = PIECES + max(map(max, LAGS))
+FIRST_ADAM = min(lags[4] for lags in LAGS)
+LAST_ADAM = max(lags[4] for lags in LAGS) + PIECES - 1
+MOVES = FIRST_ADAM - 6
 
 
 def start_row(d):
@@ -71,34 +73,6 @@
 def slot_of(color, k):
     x, y, z0, z1 = k % 2, k // 2 % 2, k // 4 % 2, k // 8
     return (x * 8 + z0 * 4 + y * 2 + z1) if color == 0 else (y * 8 + z0 * 4 + x * 2 + z1)
-
-
-def event_order():
-    loaded, rate, hop, ahead, step = LOAD_MODEL
-    ready = []
-    for at, n in LOAD:
-        for color in COLORS:
-            loaded += n * rate
-        ready.append(loaded)
-    waiting = [(ready[LOAD_OF[p]], 0, p, color) for p in range(len(PIECE)) for color in COLORS]
-    free = dict.fromkeys('xyz', 0)
-    names = ('xzyz', 'yzxz')
-    now, events = 0, []
-    while waiting:
-        def begin(e):
-            return max(now, e[0], 0 if e[1] else free[names[e[3]][0]] - ahead)
-
-        at = min(map(begin, waiting))
-        time, stage, p, color = e = max((e for e in waiting if begin(e) <= at), key=lambda e: (e[1], -e[2], -e[3]))
-        waiting.remove(e)
-        events.append(e[1:])
-        now = at + step * (1 if stage else 3)
-        if stage < 8:
-            link = names[color][min(stage, 7 - stage)]
-            rows = PIECE[p][1] * (8 >> stage if stage < 4 else (1 << stage) / GROUP)
-            free[link] = max(now, free[link]) + rows * LANES * 4 / LINK_RATE
-            waiting.append((free[link] + hop, stage + 1, p, color))
-    return events
 
 
 def big_kernel(ge, ga, gf1, gf2, gb, m_in, v_in, w_in, out_a, out_b, m_out, v_out, w_out, acc_a, acc_b, pair_a, pair_b, r1_a, r1_b, r2_a, r2_b, r3_a, r3_b, r4_a, r4_b, own_a, own_b, line_m, line_v, line_w, stage, cov, ld_sem, pr_recv, pr_send, rs_recv, rs_send, ag_recv, ag_send, loc_sem, dag_recv, dag_send, state_sem):
@@ -157,23 +131,22 @@
     def wait_on(ref, sem):
         pltpu.make_async_copy(ref, ref, sem).wait()
 
-    def add(color, into, slots, src, first, at, n):
-        @pl.loop(0, slots)
-        def _(i):
-            acc[color][into + i, pl.ds(at, n), :] += src[first + i, pl.ds(at, n), :]
+    def rows_at(p):
+        return pl.ds(pl.multiple_of(p * GROUP, GROUP), GROUP)
+
+    def add(color, into, slots, src, first, p):
+        acc[color][pl.ds(into, slots), rows_at(p), :] += src[pl.ds(first, slots), rows_at(p), :]
 
     def base(color, level):
         return sum((bits[color][i] * (TILE >> i) for i in range(level)), 0 * c)
 
     def reduce_send(color, s, p):
-        at, n = PIECE[p]
         size = TILE >> s
         first = base(color, s) + (1 - bits[color][s]) * size
-        pltpu.make_async_remote_copy(acc[color].at[pl.ds(first, size), pl.ds(at, n)], rec[color][s].at[:, pl.ds(at, n)], rs_send.at[color, s], rs_recv.at[color, s, p], device_id=routes[color][s], device_id_type=MESH).start()
+        pltpu.make_async_remote_copy(acc[color].at[pl.ds(first, size), rows_at(p)], rec[color][s].at[:, rows_at(p)], rs_send.at[color, s], rs_recv.at[color, s, p], device_id=routes[color][s], device_id_type=MESH).start()
 
     def pair_out(color, slot, size, p):
-        at, n = PIECE[p]
-        block = gat[color].at[c, pl.ds(slot, size), pl.ds(at, n)]
+        block = gat[color].at[c, pl.ds(slot, size), rows_at(p)]
         pltpu.make_async_remote_copy(block, block, dag_send.at[color], dag_recv.at[color], device_id=to_pair, device_id_type=MESH).start()
 
     def adam_block(g, load_state, store_state):
@@ -191,35 +164,31 @@
     cover_start = jnp.where(dev == LAST, LAST_START, GROUP * ((SPAN * dev) // 64))
 
     def adam(color, p):
-        at, n = PIECE[p]
         slot = base(color, 4)
-
-        @pl.loop(0, n // GROUP)
-        def _(j):
-            r = pl.multiple_of(at + j * GROUP, GROUP)
-            f = pl.multiple_of(color * HALF + r, GROUP)
-            row = cover_start + f
-            permuted = (row >= PERM_LO) & (row < PERM_HI)
-
-            def group(index):
-                for t in range(2):
-                    parts = []
-                    for q in (2 * t, 2 * t + 1):
-                        where = index(f, q)
-
-                        def keep(i, value, where=where):
-                            cov[i, where, :] = value
-
-                        parts.append(adam_block(acc[color][slot, pl.ds(r + TILE * q, TILE), :], lambda i, where=where: cov[i, where, :], keep))
-                    own[color][pl.ds(r + 16 * t, 16), :] = jnp.concatenate(parts, axis=0).astype(jnp.bfloat16)
-
-            @pl.when(permuted)
-            def _():
-                group(lambda f, q: pl.ds(f + q, TILE, stride=4))
-
-            @pl.when(jnp.logical_not(permuted))
-            def _():
-                group(lambda f, q: pl.ds(f + TILE * q, TILE))
+        r = pl.multiple_of(p * GROUP, GROUP)
+        f = pl.multiple_of(color * HALF + r, GROUP)
+        row = cover_start + f
+        permuted = (row >= PERM_LO) & (row < PERM_HI)
+
+        def group(index):
+            for t in range(2):
+                parts = []
+                for q in (2 * t, 2 * t + 1):
+                    where = index(f, q)
+
+                    def keep(i, value, where=where):
+                        cov[i, where, :] = value
+
+                    parts.append(adam_block(acc[color][slot, pl.ds(r + TILE * q, TILE), :], lambda i, where=where: cov[i, where, :], keep))
+                own[color][pl.ds(r + 16 * t, 16), :] = jnp.concatenate(parts, axis=0).astype(jnp.bfloat16)
+
+        @pl.when(permuted)
+        def _():
+            group(lambda f, q: pl.ds(f + q, TILE, stride=4))
+
+        @pl.when(jnp.logical_not(permuted))
+        def _():
+            group(lambda f, q: pl.ds(f + TILE * q, TILE))
 
     half_rows = jnp.where(dev == LAST, 115, (SPAN * dev) % 64)
     shift = half_rows // 2
@@ -239,15 +208,16 @@
             stage[i, MARGIN + 1798:MARGIN + 1799, 0:64] = lines[i][SLICE - 64:].reshape(1, 64)
 
     def state_rows_part(t):
-        @pl.loop(GROUP * t, GROUP * t + GROUP)
-        def _(j):
+        @pl.loop(0, 56)
+        def _(k):
+            j = t * 56 + k
             for i in range(3):
                 stage[i, pl.ds(pl.multiple_of(MARGIN + j * TILE, TILE), TILE), :] = lines[i][pl.ds(pl.multiple_of(j * BLOCK, BLOCK), BLOCK)].reshape(TILE, LANES)
 
     def state_to_cover(t):
-        @pl.loop(6 * t, min(6 * t + 6, ROWS // GROUP))
-        def _(j):
-            f = pl.multiple_of(j * GROUP, GROUP)
+        @pl.loop(0, -(-ROWS // GROUP // MOVES))
+        def _(k):
+            f = pl.multiple_of(jnp.minimum((t + k * MOVES) * GROUP, ROWS - GROUP), GROUP)
             r = MARGIN + f - shift
             for i in range(3):
                 here = stage[i, pl.ds(r, GROUP), :]
@@ -255,9 +225,9 @@
                 cov[i, pl.ds(f, GROUP), :] = jnp.where(c == 1, moved(before, here), here)
 
     def cover_to_state(t):
-        @pl.loop(15 * t, 15 * t + 15)
-        def _(j):
-            r = pl.multiple_of(j * TILE, TILE)
+        @pl.loop(0, 15)
+        def _(k):
+            r = pl.multiple_of((t * 15 + k) * TILE, TILE)
             for i in range(3):
                 here = cov[i, pl.ds(r + shift, TILE), :]
                 after = cov[i, pl.ds(r + shift + 1, TILE), :]
@@ -268,72 +238,87 @@
         for i, dst in enumerate((m_out, v_out, w_out)):
             pltpu.make_async_copy(stage.at[i, pl.ds(MARGIN, SLICE_ROWS)], dst, state_sem.at[i]).start()
 
-    before_adam = [state_rows] + [functools.partial(state_rows_part, t) for t in range(7)] + [functools.partial(state_to_cover, t) for t in range(10)]
-    after_adam = [functools.partial(cover_to_state, t) for t in range(15)] + [state_out]
-    adams_left = 2 * len(PIECE)
+    def start_pieces(color, p):
+        for i, (first, n) in enumerate(LOAD):
+            @pl.when(p == first // GROUP)
+            def _():
+                wait_on(acc[color].at[:, pl.ds(first, n)], ld_sem.at[color, i])
+                wait_on(pair[color].at[:, pl.ds(first, n)], pr_recv.at[color, i])
+        bit = bits[color][0]
+        for slot in ((1 - bit) * TILE, bit * TILE):
+            add(color, slot, TILE, pair[color], slot, p)
+        reduce_send(color, 0, p)
+
+    def reduce_piece(color, stage_no, p):
+        s = stage_no - 1
+        wait_on(rec[color][s].at[:, rows_at(p)], rs_recv.at[color, s, p])
+        first, size, bit = base(color, stage_no), 4 >> s, bits[color][stage_no]
+        for half in (1 - bit, bit):
+            add(color, first + half * size, size, rec[color][s], half * size, p)
+        reduce_send(color, stage_no, p)
+
+    def adam_piece(color, p):
+        wait_on(rec[color][3].at[:, rows_at(p)], rs_recv.at[color, 3, p])
+        slot = base(color, 4)
+        add(color, slot, 1, rec[color][3], 0, p)
+        adam(color, p)
+        src = own[color].at[rows_at(p)]
+        dst = gat[color].at[c, slot, rows_at(p)]
+        pltpu.make_async_remote_copy(src, dst, ag_send.at[color, 0], ag_recv.at[color, 0, p], device_id=to_z1, device_id_type=MESH).start()
+        pltpu.make_async_copy(src, dst, loc_sem.at[color, p]).start()
+        pltpu.make_async_remote_copy(src, dst, dag_send.at[color], dag_recv.at[color], device_id=to_pair, device_id_type=MESH).start()
+
+    def gather_piece(color, s, p):
+        level, size = 4 - s, 1 << s
+        bit = bits[color][level - 1]
+        arrived = base(color, level - 1) + (1 - bit) * size
+        wait_on(gat[color].at[c, pl.ds(arrived, size), rows_at(p)], ag_recv.at[color, s, p])
+        if s == 0:
+            wait_on(gat[color].at[c, base(color, 4), rows_at(p)], loc_sem.at[color, p])
+        if s < 3:
+            block = gat[color].at[c, pl.ds(base(color, level - 1), 2 * size), rows_at(p)]
+            pltpu.make_async_remote_copy(block, block, ag_send.at[color, s + 1], ag_recv.at[color, s + 1, p], device_id=routes[color][level - 2], device_id_type=MESH).start()
+        pair_out(color, arrived, size, p)
+
     load(0)
     load(1)
-    events = event_order()
-    loads_started = 2
-    waited = set()
-    for place, (stage_no, p, color) in enumerate(events):
-        at, n = PIECE[p]
-        if stage_no == 0:
-            i = LOAD_OF[p]
-            while loads_started < min(i + 2, len(LOAD)):
-                load(loads_started)
-                loads_started += 1
-            if (color, i) not in waited:
-                waited.add((color, i))
-                la, ln = LOAD[i]
-                wait_on(acc[color].at[:, pl.ds(la, ln)], ld_sem.at[color, i])
-                wait_on(pair[color].at[:, pl.ds(la, ln)], pr_recv.at[color, i])
-            away, home = (1 - bits[color][0]) * TILE, bits[color][0] * TILE
-            add(color, away, TILE, pair[color], away, at, n)
-            add(color, home, TILE, pair[color], home, at, n)
-            reduce_send(color, 0, p)
-        elif stage_no < 4:
-            s = stage_no - 1
-            size = 4 >> s
-            wait_on(rec[color][s].at[:, pl.ds(at, n)], rs_recv.at[color, s, p])
-            first = base(color, stage_no)
-            bit = bits[color][stage_no]
-            add(color, first + (1 - bit) * size, size, rec[color][s], (1 - bit) * size, at, n)
-            add(color, first + bit * size, size, rec[color][s], bit * size, at, n)
-            reduce_send(color, stage_no, p)
-        elif stage_no == 4:
-            while before_adam:
-                before_adam.pop(0)()
-            adams_left -= 1
-            wait_on(rec[color][3].at[:, pl.ds(at, n)], rs_recv.at[color, 3, p])
-            slot = base(color, 4)
-            add(color, slot, 1, rec[color][3], 0, at, n)
-            adam(color, p)
-            src = own[color].at[pl.ds(at, n)]
-            dst = gat[color].at[c, slot, pl.ds(at, n)]
-            pltpu.make_async_remote_copy(src, dst, ag_send.at[color, 0], ag_recv.at[color, 0, p], device_id=to_z1, device_id_type=MESH).start()
-            pltpu.make_async_copy(src, dst, loc_sem.at[color, p]).start()
-            pltpu.make_async_remote_copy(src, dst, dag_send.at[color], dag_recv.at[color], device_id=to_pair, device_id_type=MESH).start()
-        else:
-            s = stage_no - 5
-            level = 4 - s
-            size = 1 << s
-            bit = bits[color][level - 1]
-            arrived = base(color, level - 1) + (1 - bit) * size
-            wait_on(gat[color].at[c, pl.ds(arrived, size), pl.ds(at, n)], ag_recv.at[color, s, p])
-            if s == 0:
-                wait_on(gat[color].at[c, base(color, 4), pl.ds(at, n)], loc_sem.at[color, p])
-            if s < 3:
-                block = gat[color].at[c, pl.ds(base(color, level - 1), 2 * size), pl.ds(at, n)]
-                pltpu.make_async_remote_copy(block, block, ag_send.at[color, s + 1], ag_recv.at[color, s + 1, p], device_id=routes[color][level - 2], device_id_type=MESH).start()
-            pair_out(color, arrived, size, p)
-        if place >= 4 and before_adam:
-            before_adam.pop(0)()
-        if adams_left == 0 and after_adam:
-            after_adam.pop(0)()
-    for job in after_adam:
-        job()
-
+
+    @pl.loop(0, STEPS)
+    def _(t):
+        for i in range(2, len(LOAD)):
+            pl.when(t == LOAD[i - 1][0] // GROUP)(functools.partial(load, i))
+        for stage_no, color in SEQUENCE:
+            p = t - LAGS[color][stage_no]
+
+            @pl.when((p >= 0) & (p < PIECES))
+            def _():
+                if stage_no == 0:
+                    start_pieces(color, p)
+                elif stage_no < 4:
+                    reduce_piece(color, stage_no, p)
+                elif stage_no == 4:
+                    adam_piece(color, p)
+                else:
+                    gather_piece(color, stage_no - 5, p)
+
+        @pl.when(t == 1)
+        def _():
+            state_rows()
+
+        @pl.when((t >= 2) & (t < 6))
+        def _():
+            state_rows_part(t - 2)
+
+        @pl.when((t >= 6) & (t < FIRST_ADAM))
+        def _():
+            state_to_cover(t - 6)
+
+        @pl.when((t > LAST_ADAM) & (t <= LAST_ADAM + 15))
+        def _():
+            cover_to_state(t - LAST_ADAM - 1)
+
+    for i, dst in enumerate((m_out, v_out, w_out)):
+        pltpu.make_async_copy(stage.at[i, pl.ds(MARGIN, SLICE_ROWS)], dst, state_sem.at[i]).start()
     for i, dst in enumerate((m_out, v_out, w_out)):
         wait_on(dst, state_sem.at[i])
     for color in COLORS:
@@ -457,7 +442,6 @@
         state = (m_shard, v_shard, w_shard)
         any_spec = pl.BlockSpec(memory_space=pl.ANY)
         f32, bf16 = jnp.float32, jnp.bfloat16
-        np_ = len(PIECE)
         gathered = jax.ShapeDtypeStruct((2, 16, HALF, LANES), bf16)
         flat = jax.ShapeDtypeStruct((SLICE_ROWS, LANES), f32)
         both = lambda *shape: [pltpu.VMEM(shape, f32)] * 2
@@ -470,7 +454,7 @@
             scratch_shapes=both(16, HALF, LANES) + both(16, HALF, LANES) + both(TILE, HALF, LANES) + both(4, HALF, LANES) + both(2, HALF, LANES) + both(1, HALF, LANES)
             + [pltpu.VMEM((HALF, LANES), bf16)] * 2
             + [pltpu.VMEM((SLICE,), f32)] * 3 + [pltpu.VMEM((3, SLICE_ROWS + 2 * MARGIN, LANES), f32), pltpu.VMEM((3, COVER, LANES), f32)]
-            + [dma((2, len(LOAD))), dma((2, len(LOAD))), dma((2,)), dma((2, 4, np_)), dma((2, 4)), dma((2, 4, np_)), dma((2, 4)), dma((2, np_)), dma((2,)), dma((2,)), dma((3,))],
+            + [dma((2, len(LOAD))), dma((2, len(LOAD))), dma((2,)), dma((2, 4, PIECES)), dma((2, 4)), dma((2, 4, PIECES)), dma((2, 4)), dma((2, PIECES)), dma((2,)), dma((2,)), dma((3,))],
             compiler_params=pltpu.CompilerParams(collective_id=0, has_side_effects=True, vmem_limit_bytes=VMEM),
             name='reduce_adam_gather',
         )(*grads, *state)

time: 225 us -> 203 us (0.902)
  Pallas kernels: 221 us -> 199 us
    pallas_call x1, Pallas kernels: 203 us -> 181 us  [local_step(): pl.pallas_call(big_kernel, out_shape=(gathered, gathered, flat, flat, fla...]
where the time goes in v3:
time: 203 us
  Pallas kernels  199 us (98%)
  local copies, waits for them, and re-layouts  3.07 us (2%)
    pallas_call x1, Pallas kernels, local_step(): pl.pallas_call(big_kernel, out_shape=(gathered, gathered, flat, flat, fla...  181 us
    pallas_call x1, Pallas kernels, local_step(): pl.pallas_call(place_kernel, out_shape=[jax.ShapeDtypeStruct((n, LANES),...  17.9 us

profile of v3, /device:TPU:0, one launch (start us, length us, event | category | flops | bytes accessed | tf_op | source)
XLA Modules:
  0.0 203.0 jit_solution(9911729636151064070)
XLA Ops:
  0.6 1.5 reshape_squeeze.15.gb
  2.2 181.3 %reduce_adam_gather.1 = (bf16[2,16,928,128]{3,2,1,0:T(8,128)(2,1)}, bf16[2,16,928,128]{3,2,1,0:T(8,128)(2,1)}, f32[1800,128]{1,0:T(8,128)}, f32[1800,128]{1,0:T(8,128)}, f32[1800,128]{1,0:T(8,128)}) custom-call(f32[32768,128]{1,0:T(8,128)} %bitcast.29, f32[8192,128]{1,0:T(8,128)} %bitcast.30, f32[8192,128]{1,0:T(8,128)} %bitcast.31, f32[8192,128]{1,0:T(8,128)} %bitcast.32, ...), custom_call_target="tpu_custom_call" | custom-call | tf_op jit(solution)/shard_map/reduce_adam_gather/pallas_call | solution.py:449
  183.5 17.9 %place.1 = (bf16[32768,128]{1,0:T(8,128)(2,1)}, bf16[8192,128]{1,0:T(8,128)(2,1)}, bf16[8192,128]{1,0:T(8,128)(2,1)}, bf16[8192,128]{1,0:T(8,128)(2,1)}, bf16[20...) custom-call(bf16[2,16,928,128]{3,2,1,0:T(8,128)(2,1)} %get-tuple-ele, ...), custom_call_target="tpu_custom_call" | custom-call | tf_op jit(solution)/shard_map/place/pallas_call | solution.py:461
  201.5 1.5 reshape.61

commit v4 on v3

--- a/solution.py
+++ b/solution.py
@@ -26,13 +26,15 @@
 SLICE = 230208
 SLICE_ROWS = 1800
 MARGIN = 64
-VMEM = 62 << 20
+BIG_VMEM, PLACE_VMEM = 43 << 20, 8 << 20
 COVER = ROWS + 8
 TENSOR_ROWS = (32768, 8192, 8192, 8192, 208)
 STARTS = (0, 32768, 40960, 49152, 57344, 57552)
 PERM_LO, PERM_HI = 32768, 49152
 LOADS = (32, 64, 128, 256, 448)
 E_SLOTS = 9
+AHEAD = 3
+FRONT = AHEAD * 32
 
 
 def bounds(sizes):
@@ -75,10 +77,9 @@
     return (x * 8 + z0 * 4 + y * 2 + z1) if color == 0 else (y * 8 + z0 * 4 + x * 2 + z1)
 
 
-def big_kernel(ge, ga, gf1, gf2, gb, m_in, v_in, w_in, out_a, out_b, m_out, v_out, w_out, acc_a, acc_b, pair_a, pair_b, r1_a, r1_b, r2_a, r2_b, r3_a, r3_b, r4_a, r4_b, own_a, own_b, line_m, line_v, line_w, stage, cov, ld_sem, pr_recv, pr_send, rs_recv, rs_send, ag_recv, ag_send, loc_sem, dag_recv, dag_send, state_sem):
+def big_kernel(ge, ga, gf1, gf2, gb, m_in, v_in, w_in, gat, stage, acc_a, acc_b, pair_a, pair_b, last_a, last_b, line_m, line_v, line_w, cov, ld_sem, pr_recv, pr_send, rs_recv, rs_send, ag_recv, ag_send, dag_recv, dag_send, state_sem):
     grads = (ge, ga, gf1, gf2, gb)
-    acc, pair, own, gat = (acc_a, acc_b), (pair_a, pair_b), (own_a, own_b), (out_a, out_b)
-    rec = ((r1_a, r2_a, r3_a, r4_a), (r1_b, r2_b, r3_b, r4_b))
+    acc, pair, final = (acc_a, acc_b), (pair_a, pair_b), (last_a, last_b)
     z, y, inner = lax.axis_index('outer'), lax.axis_index('middle'), lax.axis_index('inner')
     x, c = inner // 2, inner % 2
     z0, z1 = z % 2, z // 2
@@ -106,7 +107,7 @@
         if mine:
             pltpu.make_async_copy(src, acc[color].at[slot, pl.ds(at, n)], ld_sem.at[color, i]).start()
         else:
-            pltpu.make_async_remote_copy(src, pair[color].at[slot, pl.ds(at, n)], pr_send.at[color], pr_recv.at[color, i], device_id=to_pair, device_id_type=MESH).start()
+            pltpu.make_async_remote_copy(src, pair[color].at[slot, pl.ds(FRONT + at, n)], pr_send.at[color], pr_recv.at[color, i], device_id=to_pair, device_id_type=MESH).start()
 
     def load(i):
         at, n = LOAD[i]
@@ -134,8 +135,16 @@
     def rows_at(p):
         return pl.ds(pl.multiple_of(p * GROUP, GROUP), GROUP)
 
-    def add(color, into, slots, src, first, p):
-        acc[color][pl.ds(into, slots), rows_at(p), :] += src[pl.ds(first, slots), rows_at(p), :]
+    def rows_at(p):
+        return pl.ds(pl.multiple_of(p * GROUP, GROUP), GROUP)
+
+    def add(color, into, slots, first, p, block):
+        acc[color][pl.ds(into, slots), rows_at(p), :] += pair[color][pl.ds(first, slots), rows_at(block), :]
+
+    def landing(color, s, p):
+        if s == 3:
+            return final[color].at[:, rows_at(p)]
+        return pair[color].at[pl.ds(16 - (16 >> s), TILE >> s), rows_at(p)]
 
     def base(color, level):
         return sum((bits[color][i] * (TILE >> i) for i in range(level)), 0 * c)
@@ -143,10 +152,10 @@
     def reduce_send(color, s, p):
         size = TILE >> s
         first = base(color, s) + (1 - bits[color][s]) * size
-        pltpu.make_async_remote_copy(acc[color].at[pl.ds(first, size), rows_at(p)], rec[color][s].at[:, rows_at(p)], rs_send.at[color, s], rs_recv.at[color, s, p], device_id=routes[color][s], device_id_type=MESH).start()
+        pltpu.make_async_remote_copy(acc[color].at[pl.ds(first, size), rows_at(p)], landing(color, s, p), rs_send.at[color, s], rs_recv.at[color, s, p], device_id=routes[color][s], device_id_type=MESH).start()
 
     def pair_out(color, slot, size, p):
-        block = gat[color].at[c, pl.ds(slot, size), rows_at(p)]
+        block = gat.at[color, c, pl.ds(slot, size), rows_at(p)]
         pltpu.make_async_remote_copy(block, block, dag_send.at[color], dag_recv.at[color], device_id=to_pair, device_id_type=MESH).start()
 
     def adam_block(g, load_state, store_state):
@@ -180,7 +189,7 @@
                         cov[i, where, :] = value
 
                     parts.append(adam_block(acc[color][slot, pl.ds(r + TILE * q, TILE), :], lambda i, where=where: cov[i, where, :], keep))
-                own[color][pl.ds(r + 16 * t, 16), :] = jnp.concatenate(parts, axis=0).astype(jnp.bfloat16)
+                gat[color, c, slot, pl.ds(r + 16 * t, 16), :] = jnp.concatenate(parts, axis=0).astype(jnp.bfloat16)
 
         @pl.when(permuted)
         def _():
@@ -243,41 +252,38 @@
             @pl.when(p == first // GROUP)
             def _():
                 wait_on(acc[color].at[:, pl.ds(first, n)], ld_sem.at[color, i])
-                wait_on(pair[color].at[:, pl.ds(first, n)], pr_recv.at[color, i])
+                wait_on(pair[color].at[:, pl.ds(FRONT + first, n)], pr_recv.at[color, i])
         bit = bits[color][0]
         for slot in ((1 - bit) * TILE, bit * TILE):
-            add(color, slot, TILE, pair[color], slot, p)
+            add(color, slot, TILE, slot, p, p + AHEAD)
         reduce_send(color, 0, p)
 
     def reduce_piece(color, stage_no, p):
         s = stage_no - 1
-        wait_on(rec[color][s].at[:, rows_at(p)], rs_recv.at[color, s, p])
+        wait_on(landing(color, s, p), rs_recv.at[color, s, p])
         first, size, bit = base(color, stage_no), 4 >> s, bits[color][stage_no]
         for half in (1 - bit, bit):
-            add(color, first + half * size, size, rec[color][s], half * size, p)
+            add(color, first + half * size, size, 16 - (16 >> s) + half * size, p, p)
         reduce_send(color, stage_no, p)
 
     def adam_piece(color, p):
-        wait_on(rec[color][3].at[:, rows_at(p)], rs_recv.at[color, 3, p])
+        wait_on(landing(color, 3, p), rs_recv.at[color, 3, p])
         slot = base(color, 4)
-        add(color, slot, 1, rec[color][3], 0, p)
+        acc[color][slot, rows_at(p), :] += final[color][0, rows_at(p), :]
         adam(color, p)
-        src = own[color].at[rows_at(p)]
-        dst = gat[color].at[c, slot, rows_at(p)]
-        pltpu.make_async_remote_copy(src, dst, ag_send.at[color, 0], ag_recv.at[color, 0, p], device_id=to_z1, device_id_type=MESH).start()
-        pltpu.make_async_copy(src, dst, loc_sem.at[color, p]).start()
-        pltpu.make_async_remote_copy(src, dst, dag_send.at[color], dag_recv.at[color], device_id=to_pair, device_id_type=MESH).start()
+        gather_send(color, 0, slot, 1, p)
+        pair_out(color, slot, 1, p)
+
+    def gather_send(color, s, first, size, p):
+        block = gat.at[color, c, pl.ds(first, size), rows_at(p)]
+        pltpu.make_async_remote_copy(block, block, ag_send.at[color, s], ag_recv.at[color, s, p], device_id=routes[color][3 - s], device_id_type=MESH).start()
 
     def gather_piece(color, s, p):
         level, size = 4 - s, 1 << s
-        bit = bits[color][level - 1]
-        arrived = base(color, level - 1) + (1 - bit) * size
-        wait_on(gat[color].at[c, pl.ds(arrived, size), rows_at(p)], ag_recv.at[color, s, p])
-        if s == 0:
-            wait_on(gat[color].at[c, base(color, 4), rows_at(p)], loc_sem.at[color, p])
+        arrived = base(color, level - 1) + (1 - bits[color][level - 1]) * size
+        wait_on(gat.at[color, c, pl.ds(arrived, size), rows_at(p)], ag_recv.at[color, s, p])
         if s < 3:
-            block = gat[color].at[c, pl.ds(base(color, level - 1), 2 * size), rows_at(p)]
-            pltpu.make_async_remote_copy(block, block, ag_send.at[color, s + 1], ag_recv.at[color, s + 1, p], device_id=routes[color][level - 2], device_id_type=MESH).start()
+            gather_send(color, s + 1, base(color, level - 1), 2 * size, p)
         pair_out(color, arrived, size, p)
 
     load(0)
@@ -317,68 +323,66 @@
         def _():
             cover_to_state(t - LAST_ADAM - 1)
 
-    for i, dst in enumerate((m_out, v_out, w_out)):
-        pltpu.make_async_copy(stage.at[i, pl.ds(MARGIN, SLICE_ROWS)], dst, state_sem.at[i]).start()
-    for i, dst in enumerate((m_out, v_out, w_out)):
-        wait_on(dst, state_sem.at[i])
     for color in COLORS:
-        wait_on(gat[color].at[1 - c], dag_recv.at[color])
-        wait_on(gat[color].at[c], dag_send.at[color])
+        wait_on(gat.at[color, 1 - c], dag_recv.at[color])
+        wait_on(gat.at[color, c], dag_send.at[color])
         wait_on(acc[color], pr_send.at[color])
         for s in range(4):
-            wait_on(rec[color][s], rs_send.at[color, s])
-        wait_on(own[color], ag_send.at[color, 0])
-        for s in range(1, 4):
-            wait_on(gat[color].at[0, pl.ds(0, 1 << s)], ag_send.at[color, s])
-
-
-def place_kernel(in_a, in_b, m_in, v_in, w_in, e_out, a_out, f1_out, f2_out, b_out, m_out, v_out, w_out, chip_out, buf, state, loose, vec, tail, block, in_sem, out_sem, state_sem, chip_sem):
+            wait_on(acc[color].at[pl.ds(0, TILE >> s)], rs_send.at[color, s])
+            wait_on(gat.at[color, 0, pl.ds(0, 1 << s)], ag_send.at[color, s])
+
+
+def place_kernel(gat, stage, e_out, a_out, f1_out, f2_out, b_out, m_out, v_out, w_out, chip_out, merged, loose, vec, tail, block, out_sem, edge_sem, state_sem, chip_sem):
     outs = (e_out, a_out, f1_out, f2_out, b_out)
-    ins = (in_a, in_b)
     chip = (lax.axis_index('outer') * 2 + lax.axis_index('middle')) * 2 + lax.axis_index('inner') // 2
-
-    def arriving(color, d):
-        return pltpu.make_async_copy(ins[color].at[d % 2, slot_of(color, d // 2)], buf.at[d, pl.ds(color * HALF, HALF)], in_sem.at[color, d])
-
-    for d in range(NDEV):
-        for color in COLORS:
-            arriving(color, d).start()
-    kept = [(pltpu.make_async_copy(src, state.at[i], state_sem.at[i]), pltpu.make_async_copy(state.at[i], dst, state_sem.at[i])) for i, (src, dst) in enumerate(((m_in, m_out), (v_in, v_out), (w_in, w_out)))]
-    for first, _ in kept:
-        first.start()
+    started = [pltpu.make_async_copy(stage.at[i, pl.ds(MARGIN, SLICE_ROWS)], dst, state_sem.at[i]) for i, dst in enumerate((m_out, v_out, w_out))]
+
+    def rows_from(d, at, n):
+        color = at // HALF
+        return gat.at[color, d % 2, slot_of(color, d // 2), pl.ds(at - color * HALF, n)]
+
     row = lax.broadcasted_iota(jnp.int32, (GROUP, LANES), 0)
     lane = lax.broadcasted_iota(jnp.int32, (GROUP, LANES), 1)
     tile_order = (row % TILE) * 4 + row // TILE
-    started = []
+    count = 0
     for d in range(NDEV):
+        first = merge_row(d)
+        last = merge_row(d + 1) if d < LAST else STARTS[-1]
+        begin = start_row(d)
         for color in COLORS:
-            arriving(color, d).wait()
+            lo = max(first + (GROUP if d else 0), begin + color * HALF)
+            for tensor, at, off, n in segments(lo, min(last, begin + (color + 1) * HALF) - lo):
+                started.append(pltpu.make_async_copy(rows_from(d, lo + off - begin, n), outs[tensor].at[pl.ds(at, n)], out_sem.at[count]))
+                count += 1
+    for copy in started:
+        copy.start()
+    for d in range(1, NDEV):
         first = merge_row(d)
-        last = merge_row(d + 1) if d + 1 < NDEV else STARTS[-1]
-        mine = first - start_row(d)
-        if d > 0:
-            his = first - start_row(d - 1)
-            flat = tile_order if PERM_LO <= first < PERM_HI else row
-            keep = 2 * flat + lane // 64 >= SPAN * d - 2 * first
-            new = buf[d, mine:mine + GROUP, :].astype(jnp.float32)
-            old = buf[d - 1, his:his + GROUP, :].astype(jnp.float32)
-            buf[d, mine:mine + GROUP, :] = jnp.where(keep, new, old).astype(jnp.bfloat16)
-        for tensor, at, off, n in segments(first, last - first):
-            copy = pltpu.make_async_copy(buf.at[d, pl.ds(mine + off, n)], outs[tensor].at[pl.ds(at, n)], out_sem.at[len(started)])
-            copy.start()
-            started.append(copy)
-    for first, second in kept:
-        first.wait()
-        second.start()
+        flat = tile_order if PERM_LO <= first < PERM_HI else row
+        keep = 2 * flat + lane // 64 >= SPAN * d - 2 * first
+        new, old = (rows_from(e, first - start_row(e), GROUP)[...].astype(jnp.float32) for e in (d, d - 1))
+        merged[d] = jnp.where(keep, new, old).astype(jnp.bfloat16)
+        (tensor, at, _, _), = segments(first, GROUP)
+        copy = pltpu.make_async_copy(merged.at[d], outs[tensor].at[pl.ds(at, GROUP)], edge_sem.at[d])
+        copy.start()
+        started.append(copy)
 
     def rows_of(group):
         d = (64 * group + 63) // SPAN
         begin = jnp.where(d == LAST, LAST_START, GROUP * ((SPAN * d) // 64))
-        return buf[d, pl.ds(pl.multiple_of(GROUP * group - begin, 16), GROUP), :].astype(jnp.float32)
+        k = d // 2
+        x, y, z0, z1 = k % 2, k // 2 % 2, k // 4 % 2, k // TILE
+        halves = []
+        for h in COLORS:
+            at = GROUP * group - begin + 16 * h
+            color = at // HALF
+            slot = jnp.where(color == 0, x, y) * TILE + z0 * 4 + jnp.where(color == 0, y, x) * 2 + z1
+            halves.append(gat[color, d % 2, slot, pl.ds(pl.multiple_of(at - color * HALF, 16), 16), :])
+        edge = (d > 0) & ((SPAN * d) // 64 == group)
+        return jnp.where(edge, merged[d].astype(jnp.float32), jnp.concatenate(halves, axis=0).astype(jnp.float32))
 
     def put(at, rows):
         block[0:1, pl.ds(pl.multiple_of(at * LANES, BLOCK), BLOCK)] = rows.reshape(1, BLOCK).astype(jnp.bfloat16)
-
     @pl.loop(0, 64)
     def _(j):
         rows = rows_of(chip * 64 + j)
@@ -398,7 +402,7 @@
             put(3072 + GROUP * layer + TILE * q, rows[TILE * q:TILE * q + TILE])
 
     at = STARTS[4] - start_row(LAST)
-    vec[0:208, :] = buf[LAST, at:at + 208, :].astype(jnp.float32)
+    vec[0:208, :] = rows_from(LAST, at, 208)[...].astype(jnp.float32)
     vec[208:, :] = jnp.zeros((16, LANES), jnp.float32)
     tail[...] = jnp.zeros_like(tail)
     begin = (104 * chip) % LANES
@@ -423,8 +427,6 @@
     send.start()
     for copy in started:
         copy.wait()
-    for _, second in kept:
-        second.wait()
     send.wait()
 
 
@@ -439,35 +441,30 @@
 def solution(mesh):
     def local_step(g_embed, g_attn, g_ffn_in, g_ffn_out, g_vec, m_shard, v_shard, w_shard):
         grads = (g_embed[0], tile_rows(g_attn[0]), tile_rows(g_ffn_in[0]), g_ffn_out[0].reshape(-1, LANES), g_vec[0].reshape(-1, LANES))
-        state = (m_shard, v_shard, w_shard)
-        any_spec = pl.BlockSpec(memory_space=pl.ANY)
+        any_spec, vmem_spec = pl.BlockSpec(memory_space=pl.ANY), pl.BlockSpec(memory_space=pltpu.VMEM)
         f32, bf16 = jnp.float32, jnp.bfloat16
-        gathered = jax.ShapeDtypeStruct((2, 16, HALF, LANES), bf16)
         flat = jax.ShapeDtypeStruct((SLICE_ROWS, LANES), f32)
-        both = lambda *shape: [pltpu.VMEM(shape, f32)] * 2
         dma = pltpu.SemaphoreType.DMA
-        out_a, out_b, m_new, v_new, w_new = pl.pallas_call(
+        gathered, stage = pl.pallas_call(
             big_kernel,
-            out_shape=(gathered, gathered, flat, flat, flat),
-            in_specs=[any_spec] * TILE,
-            out_specs=[any_spec] * 5,
-            scratch_shapes=both(16, HALF, LANES) + both(16, HALF, LANES) + both(TILE, HALF, LANES) + both(4, HALF, LANES) + both(2, HALF, LANES) + both(1, HALF, LANES)
-            + [pltpu.VMEM((HALF, LANES), bf16)] * 2
-            + [pltpu.VMEM((SLICE,), f32)] * 3 + [pltpu.VMEM((3, SLICE_ROWS + 2 * MARGIN, LANES), f32), pltpu.VMEM((3, COVER, LANES), f32)]
-            + [dma((2, len(LOAD))), dma((2, len(LOAD))), dma((2,)), dma((2, 4, PIECES)), dma((2, 4)), dma((2, 4, PIECES)), dma((2, 4)), dma((2, PIECES)), dma((2,)), dma((2,)), dma((3,))],
-            compiler_params=pltpu.CompilerParams(collective_id=0, has_side_effects=True, vmem_limit_bytes=VMEM),
+            out_shape=(pltpu.VMEM((2, 2, 16, HALF, LANES), bf16), pltpu.VMEM((3, SLICE_ROWS + 2 * MARGIN, LANES), f32)),
+            in_specs=[any_spec] * 8,
+            out_specs=[vmem_spec] * 2,
+            scratch_shapes=[pltpu.VMEM((16, HALF, LANES), f32)] * 2 + [pltpu.VMEM((16, HALF + FRONT, LANES), f32)] * 2 + [pltpu.VMEM((1, HALF, LANES), f32)] * 2 + [pltpu.VMEM((SLICE,), f32)] * 3 + [pltpu.VMEM((3, COVER, LANES), f32)]
+            + [dma((2, len(LOADS))), dma((2, len(LOADS))), dma((2,)), dma((2, 4, PIECES)), dma((2, 4)), dma((2, 4, PIECES)), dma((2, 4)), dma((2,)), dma((2,)), dma((3,))],
+            compiler_params=pltpu.CompilerParams(collective_id=0, has_side_effects=True, vmem_limit_bytes=BIG_VMEM),
             name='reduce_adam_gather',
-        )(*grads, *state)
+        )(*grads, m_shard, v_shard, w_shard)
         placed = pl.pallas_call(
             place_kernel,
             out_shape=[jax.ShapeDtypeStruct((n, LANES), bf16) for n in TENSOR_ROWS] + [flat] * 3 + [jax.ShapeDtypeStruct((1, 2 * SLICE), bf16)],
-            in_specs=[any_spec] * 5,
+            in_specs=[vmem_spec] * 2,
             out_specs=[any_spec] * 9,
-            scratch_shapes=[pltpu.VMEM((NDEV, ROWS, LANES), bf16), pltpu.VMEM((3, SLICE_ROWS, LANES), f32), pltpu.VMEM((2, GROUP, LANES), f32), pltpu.VMEM((224, LANES), f32), pltpu.VMEM((24, LANES), f32), pltpu.VMEM((1, 2 * SLICE), bf16)]
-            + [dma((2, NDEV)), dma((2 * NDEV,)), dma((3,)), dma(())],
-            compiler_params=pltpu.CompilerParams(vmem_limit_bytes=VMEM),
+            scratch_shapes=[pltpu.VMEM((NDEV, GROUP, LANES), bf16), pltpu.VMEM((2, GROUP, LANES), f32), pltpu.VMEM((224, LANES), f32), pltpu.VMEM((24, LANES), f32), pltpu.VMEM((1, 2 * SLICE), bf16)]
+            + [dma((2 * NDEV + TILE,)), dma((NDEV,)), dma((3,)), dma(())],
+            compiler_params=pltpu.CompilerParams(vmem_limit_bytes=PLACE_VMEM),
             name='place',
-        )(out_a, out_b, m_new, v_new, w_new)
+        )(gathered, stage)
         e, a, f1, f2, b, *state, w_chip = placed
         tensors = (e, untile(a, (16, LANES, 512)), untile(f1, (16, LANES, 512)), f2.reshape(16, 512, LANES), b.reshape(16, 1664))
         return tuple(t.reshape(-1)[:SLICE] for t in state) + tensors + (w_chip,)

time: 203 us -> 194 us (0.956)
  Pallas kernels: 199 us -> 191 us
    pallas_call x1, Pallas kernels: 17.9 us -> 10.9 us  [local_step(): pl.pallas_call(place_kernel, out_shape=[jax.ShapeDtypeStruct((n, LANES),...]
where the time goes in v4:
time: 194 us
  Pallas kernels  191 us (98%)
  local copies, waits for them, and re-layouts  2.26 us (1%)
    pallas_call x1, Pallas kernels, local_step(): pl.pallas_call(big_kernel, out_shape=(pltpu.VMEM((2, 2, 16, HALF, LANES),...  180 us
    pallas_call x1, Pallas kernels, local_step(): pl.pallas_call(place_kernel, out_shape=[jax.ShapeDtypeStruct((n, LANES),...  10.9 us

profile of v4, /device:TPU:0, one launch (start us, length us, event | category | flops | bytes accessed | tf_op | source)
XLA Modules:
  0.0 194.0 jit_solution(2017267064203178903)
XLA Ops:
  0.6 1.5 reshape_squeeze.15.gb
  2.2 180.2 %reduce_adam_gather.1 = (bf16[2,2,16,928,128]{4,3,2,1,0:T(8,128)(2,1)S(1)}, f32[3,1928,128]{2,1,0:T(8,128)S(1)}) custom-call(f32[32768,128]{1,0:T(8,128)} %bitcast.29, f32[8192,128]{1,0:T(8,128)} %bitcast.30, f32[8192,128]{1,0:T(8,128)} %bitcast.31, f32[8192,128]{1,0:T(8,128)} %bitcast.32, f32[208,128]{1,0:T(8,128)} %reshape_squeeze.15.gb, f32[230208]{0:T(1024)} %m_in.1, ...), custom_call_target="tpu_custom_call" | custom-call | tf_op jit(solution)/shard_map/reduce_adam_gather/pallas_call | solution.py:448
  182.4 10.9 %place.1 = (bf16[32768,128]{1,0:T(8,128)(2,1)}, bf16[8192,128]{1,0:T(8,128)(2,1)}, bf16[8192,128]{1,0:T(8,128)(2,1)}, bf16[8192,128]{1,0:T(8,128)(2,1)}, bf16[20...) custom-call(bf16[2,2,16,928,128]{4,3,2,1,0:T(8,128)(2,1)S(1)} %get-t, ...), custom_call_target="tpu_custom_call" | custom-call | tf_op jit(solution)/shard_map/place/pallas_call | solution.py:458
  193.3 0.7 reshape.61

commit v5 on v4

--- a/solution.py
+++ b/solution.py
@@ -30,6 +30,8 @@
 COVER = ROWS + 8
 TENSOR_ROWS = (32768, 8192, 8192, 8192, 208)
 STARTS = (0, 32768, 40960, 49152, 57344, 57552)
+VEC_TILES = 13
+INVERSE = (9329, 25)
 PERM_LO, PERM_HI = 32768, 49152
 LOADS = (32, 64, 128, 256, 448)
 E_SLOTS = 9
@@ -178,26 +180,42 @@
         f = pl.multiple_of(color * HALF + r, GROUP)
         row = cover_start + f
         permuted = (row >= PERM_LO) & (row < PERM_HI)
-
-        def group(index):
-            for t in range(2):
-                parts = []
-                for q in (2 * t, 2 * t + 1):
-                    where = index(f, q)
-
-                    def keep(i, value, where=where):
-                        cov[i, where, :] = value
-
-                    parts.append(adam_block(acc[color][slot, pl.ds(r + TILE * q, TILE), :], lambda i, where=where: cov[i, where, :], keep))
-                gat[color, c, slot, pl.ds(r + 16 * t, 16), :] = jnp.concatenate(parts, axis=0).astype(jnp.bfloat16)
+        vectors = row + GROUP > STARTS[4]
+
+        def tiles(t, index):
+            parts = []
+            for q in (2 * t, 2 * t + 1):
+                where = index(q)
+
+                def keep(i, value, where=where):
+                    cov[i, where, :] = value
+
+                parts.append(adam_block(acc[color][slot, pl.ds(r + TILE * q, TILE), :], lambda i, where=where: cov[i, where, :], keep))
+            gat[color, c, slot, pl.ds(r + 16 * t, 16), :] = jnp.concatenate(parts, axis=0).astype(jnp.bfloat16)
+
+        def plain(q):
+            return pl.ds(f + TILE * q, TILE)
+
+        def vector_tile(q):
+            tile = (row + TILE * q - STARTS[4]) // TILE
+            return pl.ds(STARTS[4] - LAST_START + tile // VEC_TILES * VEC_TILES * TILE + tile % VEC_TILES, TILE, stride=VEC_TILES)
 
         @pl.when(permuted)
         def _():
-            group(lambda f, q: pl.ds(f + q, TILE, stride=4))
-
-        @pl.when(jnp.logical_not(permuted))
-        def _():
-            group(lambda f, q: pl.ds(f + TILE * q, TILE))
+            for t in COLORS:
+                tiles(t, lambda q: pl.ds(f + q, TILE, stride=4))
+
+        @pl.when(jnp.logical_not(permuted | vectors))
+        def _():
+            for t in COLORS:
+                tiles(t, plain)
+
+        @pl.when(vectors)
+        def _():
+            for t in COLORS:
+                inside = row + 16 * t >= STARTS[4]
+                pl.when(inside)(functools.partial(tiles, t, vector_tile))
+                pl.when(jnp.logical_not(inside))(functools.partial(tiles, t, plain))
 
     half_rows = jnp.where(dev == LAST, 115, (SPAN * dev) % 64)
     shift = half_rows // 2
@@ -368,38 +386,54 @@
         started.append(copy)
 
     def rows_of(group):
-        d = (64 * group + 63) // SPAN
-        begin = jnp.where(d == LAST, LAST_START, GROUP * ((SPAN * d) // 64))
-        k = d // 2
-        x, y, z0, z1 = k % 2, k // 2 % 2, k // 4 % 2, k // TILE
+        d = (64 * group + 63) * INVERSE[0] >> INVERSE[1]
+        begin = jnp.where(d == LAST, LAST_START, (SPAN * d >> 6) * GROUP)
+        x, y, z0, z1 = ((d >> i) & 1 for i in range(1, 5))
         halves = []
         for h in COLORS:
             at = GROUP * group - begin + 16 * h
-            color = at // HALF
+            color = (at >= HALF).astype(jnp.int32)
             slot = jnp.where(color == 0, x, y) * TILE + z0 * 4 + jnp.where(color == 0, y, x) * 2 + z1
-            halves.append(gat[color, d % 2, slot, pl.ds(pl.multiple_of(at - color * HALF, 16), 16), :])
-        edge = (d > 0) & ((SPAN * d) // 64 == group)
-        return jnp.where(edge, merged[d].astype(jnp.float32), jnp.concatenate(halves, axis=0).astype(jnp.float32))
+            halves.append(gat[color, d & 1, slot, pl.ds(pl.multiple_of(at - color * HALF, 16), 16), :])
+        return halves
 
     def put(at, rows):
         block[0:1, pl.ds(pl.multiple_of(at * LANES, BLOCK), BLOCK)] = rows.reshape(1, BLOCK).astype(jnp.bfloat16)
+    def put_rows(at, halves):
+        for h, half in enumerate(halves):
+            rows = half.astype(jnp.float32)
+            for q in COLORS:
+                put(at + 16 * h + TILE * q, rows[TILE * q:TILE * q + TILE])
+
+    def put_tiles(at, halves, t):
+        for h, half in enumerate(halves):
+            rows = half.astype(jnp.float32)
+            for q in COLORS:
+                loose[t, pl.ds(2 * h + q, TILE, stride=4), :] = rows[TILE * q:TILE * q + TILE]
+        for q in range(4):
+            put(at + TILE * q, loose[t, TILE * q:TILE * q + TILE, :])
+
     @pl.loop(0, 64)
     def _(j):
-        rows = rows_of(chip * 64 + j)
-        for q in range(4):
-            put(GROUP * j + TILE * q, rows[TILE * q:TILE * q + TILE])
+        put_rows(GROUP * j, rows_of(chip * 64 + j))
 
     @pl.loop(0, 16)
     def _(layer):
         for t in (1, 2):
-            rows = rows_of(STARTS[t] // GROUP + layer * 16 + chip)
-            for q in range(4):
-                loose[t - 1, pl.ds(q, TILE, stride=4), :] = rows[TILE * q:TILE * q + TILE]
-            for q in range(4):
-                put(1536 + 512 * t + GROUP * layer + TILE * q, loose[t - 1, TILE * q:TILE * q + TILE, :])
-        rows = rows_of(STARTS[3] // GROUP + layer * 16 + chip)
-        for q in range(4):
-            put(3072 + GROUP * layer + TILE * q, rows[TILE * q:TILE * q + TILE])
+            put_tiles(1536 + 512 * t + GROUP * layer, rows_of(STARTS[t] // GROUP + layer * 16 + chip), t - 1)
+        put_rows(3072 + GROUP * layer, rows_of(STARTS[3] // GROUP + layer * 16 + chip))
+
+    for d in range(1, NDEV):
+        (tensor, at, _, _), = segments(merge_row(d), GROUP)
+        layer, owner = divmod(at // GROUP, 16)
+
+        @pl.when(chip == (owner if tensor else at // 2048))
+        def _():
+            halves = (merged[d, 0:16, :], merged[d, 16:, :])
+            if tensor in (1, 2):
+                put_tiles(1536 + 512 * tensor + GROUP * layer, halves, tensor - 1)
+            else:
+                put_rows(3072 + GROUP * layer if tensor else at % 2048, halves)
 
     at = STARTS[4] - start_row(LAST)
     vec[0:208, :] = rows_from(LAST, at, 208)[...].astype(jnp.float32)
@@ -408,12 +442,12 @@
     begin = (104 * chip) % LANES
     line = lax.broadcasted_iota(jnp.int32, (TILE, LANES), 1)
     for layer in range(16):
-        source = layer * 13 + (104 * chip) // LANES
+        source = layer // TILE * TILE * VEC_TILES + layer % TILE + (104 * chip) // LANES * TILE
         to = layer * 104 // LANES
         off = layer * 104 % LANES
         turn = (off - begin + LANES) % LANES
         one = pltpu.roll(vec[pl.ds(source, TILE), :], turn, 1)
-        two = pltpu.roll(vec[pl.ds(source + 1, TILE), :], turn, 1)
+        two = pltpu.roll(vec[pl.ds(source + TILE, TILE), :], turn, 1)
         t = (line - off + LANES) % LANES
         got = jnp.where(begin + t < LANES, one, two)
         here = (t < 104) & (line >= off)
@@ -430,17 +464,17 @@
     send.wait()
 
 
-def tile_rows(tensor):
-    return tensor.reshape(-1, TILE, 4, LANES).transpose(0, 2, 1, 3).reshape(-1, LANES)
-
-
-def untile(rows, shape):
-    return rows.reshape(-1, 4, TILE, LANES).transpose(0, 2, 1, 3).reshape(shape)
+def tile_rows(tensor, tiles=4):
+    return tensor.reshape(-1, TILE, tiles, LANES).transpose(0, 2, 1, 3).reshape(-1, LANES)
+
+
+def untile(rows, shape, tiles=4):
+    return rows.reshape(-1, tiles, TILE, LANES).transpose(0, 2, 1, 3).reshape(shape)
 
 
 def solution(mesh):
     def local_step(g_embed, g_attn, g_ffn_in, g_ffn_out, g_vec, m_shard, v_shard, w_shard):
-        grads = (g_embed[0], tile_rows(g_attn[0]), tile_rows(g_ffn_in[0]), g_ffn_out[0].reshape(-1, LANES), g_vec[0].reshape(-1, LANES))
+        grads = (g_embed[0], tile_rows(g_attn[0]), tile_rows(g_ffn_in[0]), g_ffn_out[0].reshape(-1, LANES), tile_rows(g_vec[0], VEC_TILES))
         any_spec, vmem_spec = pl.BlockSpec(memory_space=pl.ANY), pl.BlockSpec(memory_space=pltpu.VMEM)
         f32, bf16 = jnp.float32, jnp.bfloat16
         flat = jax.ShapeDtypeStruct((SLICE_ROWS, LANES), f32)
@@ -466,7 +500,7 @@
             name='place',
         )(gathered, stage)
         e, a, f1, f2, b, *state, w_chip = placed
-        tensors = (e, untile(a, (16, LANES, 512)), untile(f1, (16, LANES, 512)), f2.reshape(16, 512, LANES), b.reshape(16, 1664))
+        tensors = (e, untile(a, (16, LANES, 512)), untile(f1, (16, LANES, 512)), f2.reshape(16, 512, LANES), untile(b, (16, 1664), VEC_TILES))
         return tuple(t.reshape(-1)[:SLICE] for t in state) + tensors + (w_chip,)
 
     return jax.shard_map(local_step, mesh=mesh, in_specs=(P(MESH_AXES),) * TILE, out_specs=(P(MESH_AXES),) * 3 + (P(),) * 5 + (P(MESH_AXES),), check_vma=False)

time: 194 us -> 188 us (0.969)
  Pallas kernels: 191 us -> 188 us
  local copies, waits for them, and re-layouts: 2.26 us -> 0 us
    pallas_call x1, Pallas kernels: 10.9 us -> 7.61 us  [local_step(): pl.pallas_call(place_kernel, out_shape=[jax.ShapeDtypeStruct((n, LANES),...]
where the time goes in v5:
time: 188 us
  Pallas kernels  188 us (100%)
    pallas_call x1, Pallas kernels, local_step(): pl.pallas_call(big_kernel, out_shape=(pltpu.VMEM((2, 2, 16, HALF, LANES),...  180 us
    pallas_call x1, Pallas kernels, local_step(): pl.pallas_call(place_kernel, out_shape=[jax.ShapeDtypeStruct((n, LANES),...  7.61 us

profile of v5, /device:TPU:0, one launch (start us, length us, event | category | flops | bytes accessed | tf_op | source)
XLA Modules:
  0.0 188.3 jit_solution(17557490226677602396)
XLA Ops:
  0.6 180.0 %reduce_adam_gather.1 = (bf16[2,2,16,928,128]{4,3,2,1,0:T(8,128)(2,1)S(1)}, f32[3,1928,128]{2,1,0:T(8,128)S(1)}) custom-call(f32[32768,128]{1,0:T(8,128)} %bitcast.39, f32[8192,128]{1,0:T(8,128)} %bitcast.40, f32[8192,128]{1,0:T(8,128)} %bitcast.41, f32[8192,128]{1,0:T(8,128)} %bitcast.42, f32[208,128]{1,0:T(8,128)} %bitcast.43, f32[230208]{0:T(1024)} %m_in.1, ...), custom_call_target="tpu_custom_call" | custom-call | tf_op jit(solution)/shard_map/reduce_adam_gather/pallas_call | solution.py:482
  180.6 7.6 %place.1 = (bf16[32768,128]{1,0:T(8,128)(2,1)}, bf16[8192,128]{1,0:T(8,128)(2,1)}, bf16[8192,128]{1,0:T(8,128)(2,1)}, bf16[8192,128]{1,0:T(8,128)(2,1)}, bf16[20...) custom-call(bf16[2,2,16,928,128]{4,3,2,1,0:T(8,128)(2,1)S(1)} %get-t, ...), custom_call_target="tpu_custom_call" | custom-call | tf_op jit(solution)/shard_map/place/pallas_call | solution.py:492

commit v6 on v5

--- a/solution.py
+++ b/solution.py
@@ -33,9 +33,10 @@
 VEC_TILES = 13
 INVERSE = (9329, 25)
 PERM_LO, PERM_HI = 32768, 49152
-LOADS = (32, 64, 128, 256, 448)
+LOADS = (32, 64, 128, 256, 288, 160)
 E_SLOTS = 9
-AHEAD = 3
+LATE = 24
+AHEAD = 4
 FRONT = AHEAD * 32
 
 
@@ -49,8 +50,8 @@
 
 LOAD = bounds(LOADS)
 PIECES = HALF // GROUP
-LAGS = ((0, 3, 6, 8, 12, 19, 32, 36, 53), (0, 3, 6, 10, 16, 20, 31, 35, 52))
-SEQUENCE = ((8, 0), (6, 0), (8, 1), (7, 0), (2, 0), (3, 1), (1, 0), (0, 0), (5, 1), (5, 0), (4, 1), (6, 1), (4, 0), (2, 1), (1, 1), (0, 1), (3, 0), (7, 1))
+LAGS = ((0, 3, 6, 9, 14, 20, 25, 29, 41), (0, 3, 6, 10, 16, 20, 24, 30, 45))
+SEQUENCE = ((0, 0), (8, 1), (4, 1), (5, 0), (3, 1), (6, 0), (7, 1), (1, 0), (2, 1), (3, 0), (8, 0), (7, 0), (4, 0), (1, 1), (5, 1), (2, 0), (0, 1), (6, 1))
 STEPS = PIECES + max(map(max, LAGS))
 FIRST_ADAM = min(lags[4] for lags in LAGS)
 LAST_ADAM = max(lags[4] for lags in LAGS) + PIECES - 1
@@ -74,9 +75,10 @@
     return out
 
 
-def slot_of(color, k):
+def slot_of(color, k, late=False):
     x, y, z0, z1 = k % 2, k // 2 % 2, k // 4 % 2, k // 8
-    return (x * 8 + z0 * 4 + y * 2 + z1) if color == 0 else (y * 8 + z0 * 4 + x * 2 + z1)
+    first, third = (x, y) if color == 0 else (y, x)
+    return first * 8 + (third * 4 + z0 * 2 if late else z0 * 4 + third * 2) + z1
 
 
 def big_kernel(ge, ga, gf1, gf2, gb, m_in, v_in, w_in, gat, stage, acc_a, acc_b, pair_a, pair_b, last_a, last_b, line_m, line_v, line_w, cov, ld_sem, pr_recv, pr_send, rs_recv, rs_send, ag_recv, ag_send, dag_recv, dag_send, state_sem):
@@ -116,7 +118,7 @@
         for color in COLORS:
             @pl.loop(0, E_SLOTS)
             def _(k):
-                slot = slot_of(color, k)
+                slot = slot_of(color, k, at >= LATE * GROUP)
                 for mine in (False, True):
                     d = 2 * k + (c if mine else 1 - c)
                     row = pl.multiple_of(GROUP * ((SPAN * d) // 64), GROUP) + color * HALF + at
@@ -125,7 +127,7 @@
                 @pl.when(c == core)
                 def _():
                     for k in range(E_SLOTS, NDEV // 2):
-                        slot = slot_of(color, k)
+                        slot = slot_of(color, k, at >= LATE * GROUP)
                         for mine in (False, True):
                             d = 2 * k + (core if mine else 1 - core)
                             for tensor, row, off, rows in segments(start_row(d) + color * HALF + at, n):
@@ -151,10 +153,25 @@
     def base(color, level):
         return sum((bits[color][i] * (TILE >> i) for i in range(level)), 0 * c)
 
+    def halved(color, level, p):
+        one, other = bits[color][level], bits[color][3 - level if level in (1, 2) else level]
+        return jnp.where(p >= LATE, other, one)
+
+    def reduce_base(color, level, p):
+        return sum((halved(color, i, p) * (TILE >> i) for i in range(level)), 0 * c)
+
+    def reduce_to(color, s, p):
+        if s in (0, 3):
+            return routes[color][s]
+        along_z = p < LATE if s == 1 else p >= LATE
+        across_y = jnp.logical_not(along_z) & (color == 0)
+        across_x = jnp.logical_not(along_z) & (color == 1)
+        return {'outer': jnp.where(along_z, to_z0['outer'], z), 'middle': jnp.where(across_y, 1 - y, y), 'inner': jnp.where(across_x, to_x['inner'], inner)}
+
     def reduce_send(color, s, p):
         size = TILE >> s
-        first = base(color, s) + (1 - bits[color][s]) * size
-        pltpu.make_async_remote_copy(acc[color].at[pl.ds(first, size), rows_at(p)], landing(color, s, p), rs_send.at[color, s], rs_recv.at[color, s, p], device_id=routes[color][s], device_id_type=MESH).start()
+        first = reduce_base(color, s, p) + (1 - halved(color, s, p)) * size
+        pltpu.make_async_remote_copy(acc[color].at[pl.ds(first, size), rows_at(p)], landing(color, s, p), rs_send.at[color, s], rs_recv.at[color, s, p], device_id=reduce_to(color, s, p), device_id_type=MESH).start()
 
     def pair_out(color, slot, size, p):
         block = gat.at[color, c, pl.ds(slot, size), rows_at(p)]
@@ -175,7 +192,7 @@
     cover_start = jnp.where(dev == LAST, LAST_START, GROUP * ((SPAN * dev) // 64))
 
     def adam(color, p):
-        slot = base(color, 4)
+        slot, summed = base(color, 4), reduce_base(color, 4, p)
         r = pl.multiple_of(p * GROUP, GROUP)
         f = pl.multiple_of(color * HALF + r, GROUP)
         row = cover_start + f
@@ -190,7 +207,7 @@
                 def keep(i, value, where=where):
                     cov[i, where, :] = value
 
-                parts.append(adam_block(acc[color][slot, pl.ds(r + TILE * q, TILE), :], lambda i, where=where: cov[i, where, :], keep))
+                parts.append(adam_block(acc[color][summed, pl.ds(r + TILE * q, TILE), :], lambda i, where=where: cov[i, where, :], keep))
             gat[color, c, slot, pl.ds(r + 16 * t, 16), :] = jnp.concatenate(parts, axis=0).astype(jnp.bfloat16)
 
         def plain(q):
@@ -279,7 +296,7 @@
     def reduce_piece(color, stage_no, p):
         s = stage_no - 1
         wait_on(landing(color, s, p), rs_recv.at[color, s, p])
-        first, size, bit = base(color, stage_no), 4 >> s, bits[color][stage_no]
+        first, size, bit = reduce_base(color, stage_no, p), 4 >> s, halved(color, stage_no, p)
         for half in (1 - bit, bit):
             add(color, first + half * size, size, 16 - (16 >> s) + half * size, p, p)
         reduce_send(color, stage_no, p)
@@ -287,7 +304,7 @@
     def adam_piece(color, p):
         wait_on(landing(color, 3, p), rs_recv.at[color, 3, p])
         slot = base(color, 4)
-        acc[color][slot, rows_at(p), :] += final[color][0, rows_at(p), :]
+        acc[color][reduce_base(color, 4, p), rows_at(p), :] += final[color][0, rows_at(p), :]
         adam(color, p)
         gather_send(color, 0, slot, 1, p)
         pair_out(color, slot, 1, p)
@@ -305,7 +322,6 @@
         pair_out(color, arrived, size, p)
 
     load(0)
-    load(1)
 
     @pl.loop(0, STEPS)
     def _(t):
@@ -324,6 +340,8 @@
                     adam_piece(color, p)
                 else:
                     gather_piece(color, stage_no - 5, p)
+
+        pl.when(t == 0)(functools.partial(load, 1))
 
         @pl.when(t == 1)
         def _():

time: 188 us -> 185 us (0.984)
  Pallas kernels: 188 us -> 185 us
    pallas_call x1, Pallas kernels: 180 us -> 177 us  [local_step(): pl.pallas_call(big_kernel, out_shape=(pltpu.VMEM((2, 2, 16, HALF, LANES),...]
where the time goes in v6:
time: 185 us
  Pallas kernels  185 us (100%)
    pallas_call x1, Pallas kernels, local_step(): pl.pallas_call(big_kernel, out_shape=(pltpu.VMEM((2, 2, 16, HALF, LANES),...  177 us
    pallas_call x1, Pallas kernels, local_step(): pl.pallas_call(place_kernel, out_shape=[jax.ShapeDtypeStruct((n, LANES),...  7.61 us

profile of v6, /device:TPU:0, one launch (start us, length us, event | category | flops | bytes accessed | tf_op | source)
XLA Modules:
  0.0 185.2 jit_solution(13027341400017532281)
XLA Ops:
  0.6 176.9 %reduce_adam_gather.1 = (bf16[2,2,16,928,128]{4,3,2,1,0:T(8,128)(2,1)S(1)}, f32[3,1928,128]{2,1,0:T(8,128)S(1)}) custom-call(f32[32768,128]{1,0:T(8,128)} %bitcast.39, f32[8192,128]{1,0:T(8,128)} %bitcast.40, f32[8192,128]{1,0:T(8,128)} %bitcast.41, f32[8192,128]{1,0:T(8,128)} %bitcast.42, f32[208,128]{1,0:T(8,128)} %bitcast.43, f32[230208]{0:T(1024)} %m_in.1, ...), custom_call_target="tpu_custom_call" | custom-call | tf_op jit(solution)/shard_map/reduce_adam_gather/pallas_call | solution.py:500
  177.6 7.6 %place.1 = (bf16[32768,128]{1,0:T(8,128)(2,1)}, bf16[8192,128]{1,0:T(8,128)(2,1)}, bf16[8192,128]{1,0:T(8,128)(2,1)}, bf16[8192,128]{1,0:T(8,128)(2,1)}, bf16[20...) custom-call(bf16[2,2,16,928,128]{4,3,2,1,0:T(8,128)(2,1)S(1)} %get-t, ...), custom_call_target="tpu_custom_call" | custom-call | tf_op jit(solution)/shard_map/place/pallas_call | solution.py:510

commit v7 on v6

--- a/solution.py
+++ b/solution.py
@@ -35,6 +35,7 @@
 PERM_LO, PERM_HI = 32768, 49152
 LOADS = (32, 64, 128, 256, 288, 160)
 E_SLOTS = 9
+E_ROWS = 2048
 LATE = 24
 AHEAD = 4
 FRONT = AHEAD * 32
@@ -100,12 +101,6 @@
     for to in (to_pair, to_x, to_y, to_z0, to_z1):
         pl.semaphore_signal(barrier, inc=1, device_id=to, device_id_type=MESH)
 
-    lines = (line_m, line_v, line_w)
-    state_in = [pltpu.make_async_copy(src, lines[i], state_sem.at[i]) for i, src in enumerate((m_in, v_in, w_in))]
-    for copy in state_in:
-        copy.start()
-    pl.semaphore_wait(barrier, 5)
-
     def load_one(color, i, tensor, row, slot, at, n, mine):
         src = grads[tensor].at[pl.ds(row, n)]
         if mine:
@@ -113,13 +108,13 @@
         else:
             pltpu.make_async_remote_copy(src, pair[color].at[slot, pl.ds(FRONT + at, n)], pr_send.at[color], pr_recv.at[color, i], device_id=to_pair, device_id_type=MESH).start()
 
-    def load(i):
+    def load(i, sides=(True, False)):
         at, n = LOAD[i]
         for color in COLORS:
             @pl.loop(0, E_SLOTS)
             def _(k):
                 slot = slot_of(color, k, at >= LATE * GROUP)
-                for mine in (False, True):
+                for mine in sides:
                     d = 2 * k + (c if mine else 1 - c)
                     row = pl.multiple_of(GROUP * ((SPAN * d) // 64), GROUP) + color * HALF + at
                     load_one(color, i, 0, row, slot, at, n, mine)
@@ -128,10 +123,17 @@
                 def _():
                     for k in range(E_SLOTS, NDEV // 2):
                         slot = slot_of(color, k, at >= LATE * GROUP)
-                        for mine in (False, True):
+                        for mine in sides:
                             d = 2 * k + (core if mine else 1 - core)
                             for tensor, row, off, rows in segments(start_row(d) + color * HALF + at, n):
                                 load_one(color, i, tensor, row, slot, at + off, rows, mine)
+
+    load(0, (True,))
+    lines = (line_m, line_v, line_w)
+    state_in = [pltpu.make_async_copy(src, lines[i], state_sem.at[i]) for i, src in enumerate((m_in, v_in, w_in))]
+    for copy in state_in:
+        copy.start()
+    pl.semaphore_wait(barrier, 5)
 
     def wait_on(ref, sem):
         pltpu.make_async_copy(ref, ref, sem).wait()
@@ -321,7 +323,7 @@
             gather_send(color, s + 1, base(color, level - 1), 2 * size, p)
         pair_out(color, arrived, size, p)
 
-    load(0)
+    load(0, (False,))
 
     @pl.loop(0, STEPS)
     def _(t):
@@ -431,28 +433,37 @@
         for q in range(4):
             put(at + TILE * q, loose[t, TILE * q:TILE * q + TILE, :])
 
-    @pl.loop(0, 64)
+    def put_edges(tensors):
+        for d in range(1, NDEV):
+            (tensor, at, _, _), = segments(merge_row(d), GROUP)
+            if tensor not in tensors:
+                continue
+            layer, owner = divmod(at // GROUP, 16)
+
+            @pl.when(chip == (owner if tensor else at // E_ROWS))
+            def _():
+                halves = (merged[d, 0:16, :], merged[d, 16:, :])
+                if tensor in (1, 2):
+                    put_tiles(1536 + 512 * tensor + GROUP * layer, halves, tensor - 1)
+                else:
+                    put_rows(3072 + GROUP * layer if tensor else at % E_ROWS, halves)
+
+    @pl.loop(0, 64, unroll=4)
     def _(j):
         put_rows(GROUP * j, rows_of(chip * 64 + j))
 
-    @pl.loop(0, 16)
+    put_edges((0,))
+    split = E_ROWS * LANES
+    sends = [pltpu.make_async_copy(block.at[:, pl.ds(at, n)], chip_out.at[:, pl.ds(at, n)], chip_sem.at[i]) for i, (at, n) in enumerate(((0, split), (split, 2 * SLICE - split)))]
+    sends[0].start()
+
+    @pl.loop(0, 16, unroll=2)
     def _(layer):
         for t in (1, 2):
             put_tiles(1536 + 512 * t + GROUP * layer, rows_of(STARTS[t] // GROUP + layer * 16 + chip), t - 1)
         put_rows(3072 + GROUP * layer, rows_of(STARTS[3] // GROUP + layer * 16 + chip))
 
-    for d in range(1, NDEV):
-        (tensor, at, _, _), = segments(merge_row(d), GROUP)
-        layer, owner = divmod(at // GROUP, 16)
-
-        @pl.when(chip == (owner if tensor else at // 2048))
-        def _():
-            halves = (merged[d, 0:16, :], merged[d, 16:, :])
-            if tensor in (1, 2):
-                put_tiles(1536 + 512 * tensor + GROUP * layer, halves, tensor - 1)
-            else:
-                put_rows(3072 + GROUP * layer if tensor else at % 2048, halves)
-
+    put_edges((1, 2, 3))
     at = STARTS[4] - start_row(LAST)
     vec[0:208, :] = rows_from(LAST, at, 208)[...].astype(jnp.float32)
     vec[208:, :] = jnp.zeros((16, LANES), jnp.float32)
@@ -475,11 +486,9 @@
             tail[to + 1:to + 2, :] = jnp.where(there, got, tail[pl.ds(to + 1, TILE), :])[0:1]
     put(3584, tail[0:TILE, :])
     block[0:1, 3592 * LANES:] = tail[TILE:16, :].reshape(1, BLOCK)[:, 0:640].astype(jnp.bfloat16)
-    send = pltpu.make_async_copy(block, chip_out, chip_sem)
-    send.start()
-    for copy in started:
+    sends[1].start()
+    for copy in started + sends:
         copy.wait()
-    send.wait()
 
 
 def tile_rows(tensor, tiles=4):
@@ -513,7 +522,7 @@
             in_specs=[vmem_spec] * 2,
             out_specs=[any_spec] * 9,
             scratch_shapes=[pltpu.VMEM((NDEV, GROUP, LANES), bf16), pltpu.VMEM((2, GROUP, LANES), f32), pltpu.VMEM((224, LANES), f32), pltpu.VMEM((24, LANES), f32), pltpu.VMEM((1, 2 * SLICE), bf16)]
-            + [dma((2 * NDEV + TILE,)), dma((NDEV,)), dma((3,)), dma(())],
+            + [dma((2 * NDEV + TILE,)), dma((NDEV,)), dma((3,)), dma((2,))],
             compiler_params=pltpu.CompilerParams(vmem_limit_bytes=PLACE_VMEM),
             name='place',
         )(gathered, stage)

time: 185 us -> 186 us (level)
  no operation moved by 1% of the time
where the time goes in v7:
time: 186 us
  Pallas kernels  185 us (99%)
    pallas_call x1, Pallas kernels, local_step(): pl.pallas_call(big_kernel, out_shape=(pltpu.VMEM((2, 2, 16, HALF, LANES),...  177 us
    pallas_call x1, Pallas kernels, local_step(): pl.pallas_call(place_kernel, out_shape=[jax.ShapeDtypeStruct((n, LANES),...  7.59 us

profile of v7, /device:TPU:0, one launch (start us, length us, event | category | flops | bytes accessed | tf_op | source)
XLA Modules:
  0.0 185.6 jit_solution(12619833029824043004)
XLA Ops:
  0.6 177.3 %reduce_adam_gather.1 = (bf16[2,2,16,928,128]{4,3,2,1,0:T(8,128)(2,1)S(1)}, f32[3,1928,128]{2,1,0:T(8,128)S(1)}) custom-call(f32[32768,128]{1,0:T(8,128)} %bitcast.39, f32[8192,128]{1,0:T(8,128)} %bitcast.40, f32[8192,128]{1,0:T(8,128)} %bitcast.41, f32[8192,128]{1,0:T(8,128)} %bitcast.42, f32[208,128]{1,0:T(8,128)} %bitcast.43, f32[230208]{0:T(1024)} %m_in.1, ...), custom_call_target="tpu_custom_call" | custom-call | tf_op jit(solution)/shard_map/reduce_adam_gather/pallas_call | solution.py:509
  178.0 7.6 %place.1 = (bf16[32768,128]{1,0:T(8,128)(2,1)}, bf16[8192,128]{1,0:T(8,128)(2,1)}, bf16[8192,128]{1,0:T(8,128)(2,1)}, bf16[8192,128]{1,0:T(8,128)(2,1)}, bf16[20...) custom-call(bf16[2,2,16,928,128]{4,3,2,1,0:T(8,128)(2,1)S(1)} %get-t, ...), custom_call_target="tpu_custom_call" | custom-call | tf_op jit(solution)/shard_map/place/pallas_call | solution.py:519

commit v8 on v7

--- a/solution.py
+++ b/solution.py
@@ -309,7 +309,6 @@
         acc[color][reduce_base(color, 4, p), rows_at(p), :] += final[color][0, rows_at(p), :]
         adam(color, p)
         gather_send(color, 0, slot, 1, p)
-        pair_out(color, slot, 1, p)
 
     def gather_send(color, s, first, size, p):
         block = gat.at[color, c, pl.ds(first, size), rows_at(p)]
@@ -321,7 +320,8 @@
         wait_on(gat.at[color, c, pl.ds(arrived, size), rows_at(p)], ag_recv.at[color, s, p])
         if s < 3:
             gather_send(color, s + 1, base(color, level - 1), 2 * size, p)
-        pair_out(color, arrived, size, p)
+        if s > 1:
+            pair_out(color, arrived if s == 3 else base(color, 1), TILE, p)
 
     load(0, (False,))
 

time: 186 us -> 185 us (level)
  no operation moved by 1% of the time
where the time goes in v8:
time: 185 us
  Pallas kernels  184 us (99%)
    pallas_call x1, Pallas kernels, local_step(): pl.pallas_call(big_kernel, out_shape=(pltpu.VMEM((2, 2, 16, HALF, LANES),...  176 us
    pallas_call x1, Pallas kernels, local_step(): pl.pallas_call(place_kernel, out_shape=[jax.ShapeDtypeStruct((n, LANES),...  7.59 us

profile of v8, /device:TPU:0, one launch (start us, length us, event | category | flops | bytes accessed | tf_op | source)
XLA Modules:
  0.0 184.6 jit_solution(1617984615605860246)
XLA Ops:
  0.6 176.4 %reduce_adam_gather.1 = (bf16[2,2,16,928,128]{4,3,2,1,0:T(8,128)(2,1)S(1)}, f32[3,1928,128]{2,1,0:T(8,128)S(1)}) custom-call(f32[32768,128]{1,0:T(8,128)} %bitcast.39, f32[8192,128]{1,0:T(8,128)} %bitcast.40, f32[8192,128]{1,0:T(8,128)} %bitcast.41, f32[8192,128]{1,0:T(8,128)} %bitcast.42, f32[208,128]{1,0:T(8,128)} %bitcast.43, f32[230208]{0:T(1024)} %m_in.1, ...), custom_call_target="tpu_custom_call" | custom-call | tf_op jit(solution)/shard_map/reduce_adam_gather/pallas_call | solution.py:509
  177.0 7.6 %place.1 = (bf16[32768,128]{1,0:T(8,128)(2,1)}, bf16[8192,128]{1,0:T(8,128)(2,1)}, bf16[8192,128]{1,0:T(8,128)(2,1)}, bf16[8192,128]{1,0:T(8,128)(2,1)}, bf16[20...) custom-call(bf16[2,2,16,928,128]{4,3,2,1,0:T(8,128)(2,1)S(1)} %get-t, ...), custom_call_target="tpu_custom_call" | custom-call | tf_op jit(solution)/shard_map/place/pallas_call | solution.py:519

commit v9 on v8

--- a/solution.py
+++ b/solution.py
@@ -33,10 +33,10 @@
 VEC_TILES = 13
 INVERSE = (9329, 25)
 PERM_LO, PERM_HI = 32768, 49152
-LOADS = (32, 64, 128, 256, 288, 160)
+LOADS = (32, 64, 128, 256, 256, 192)
 E_SLOTS = 9
 E_ROWS = 2048
-LATE = 24
+LATE = 23
 AHEAD = 4
 FRONT = AHEAD * 32
 
@@ -51,8 +51,8 @@
 
 LOAD = bounds(LOADS)
 PIECES = HALF // GROUP
-LAGS = ((0, 3, 6, 9, 14, 20, 25, 29, 41), (0, 3, 6, 10, 16, 20, 24, 30, 45))
-SEQUENCE = ((0, 0), (8, 1), (4, 1), (5, 0), (3, 1), (6, 0), (7, 1), (1, 0), (2, 1), (3, 0), (8, 0), (7, 0), (4, 0), (1, 1), (5, 1), (2, 0), (0, 1), (6, 1))
+LAGS = ((0, 3, 6, 9, 15, 20, 25, 29, 33), (0, 3, 5, 8, 14, 19, 24, 29, 33))
+SEQUENCE = ((8, 0), (7, 1), (4, 1), (6, 0), (1, 1), (0, 0), (4, 0), (3, 1), (1, 0), (0, 1), (2, 0), (6, 1), (5, 1), (2, 1), (5, 0), (7, 0), (8, 1), (3, 0))
 STEPS = PIECES + max(map(max, LAGS))
 FIRST_ADAM = min(lags[4] for lags in LAGS)
 LAST_ADAM = max(lags[4] for lags in LAGS) + PIECES - 1

time: 185 us -> 182 us (0.984)
  Pallas kernels: 184 us -> 181 us
    pallas_call x1, Pallas kernels: 176 us -> 173 us  [local_step(): pl.pallas_call(big_kernel, out_shape=(pltpu.VMEM((2, 2, 16, HALF, LANES),...]
where the time goes in v9:
time: 182 us
  Pallas kernels  181 us (99%)
    pallas_call x1, Pallas kernels, local_step(): pl.pallas_call(big_kernel, out_shape=(pltpu.VMEM((2, 2, 16, HALF, LANES),...  173 us
    pallas_call x1, Pallas kernels, local_step(): pl.pallas_call(place_kernel, out_shape=[jax.ShapeDtypeStruct((n, LANES),...  7.59 us

profile of v9, /device:TPU:0, one launch (start us, length us, event | category | flops | bytes accessed | tf_op | source)
XLA Modules:
  0.0 181.6 jit_solution(4552692167774274562)
XLA Ops:
  0.6 173.3 %reduce_adam_gather.1 = (bf16[2,2,16,928,128]{4,3,2,1,0:T(8,128)(2,1)S(1)}, f32[3,1928,128]{2,1,0:T(8,128)S(1)}) custom-call(f32[32768,128]{1,0:T(8,128)} %bitcast.39, f32[8192,128]{1,0:T(8,128)} %bitcast.40, f32[8192,128]{1,0:T(8,128)} %bitcast.41, f32[8192,128]{1,0:T(8,128)} %bitcast.42, f32[208,128]{1,0:T(8,128)} %bitcast.43, f32[230208]{0:T(1024)} %m_in.1, ...), custom_call_target="tpu_custom_call" | custom-call | tf_op jit(solution)/shard_map/reduce_adam_gather/pallas_call | solution.py:509
  174.0 7.6 %place.1 = (bf16[32768,128]{1,0:T(8,128)(2,1)}, bf16[8192,128]{1,0:T(8,128)(2,1)}, bf16[8192,128]{1,0:T(8,128)(2,1)}, bf16[8192,128]{1,0:T(8,128)(2,1)}, bf16[20...) custom-call(bf16[2,2,16,928,128]{4,3,2,1,0:T(8,128)(2,1)S(1)} %get-t, ...), custom_call_target="tpu_custom_call" | custom-call | tf_op jit(solution)/shard_map/place/pallas_call | solution.py:519

commit v10 on v9

--- a/solution.py
+++ b/solution.py
@@ -51,8 +51,8 @@
 
 LOAD = bounds(LOADS)
 PIECES = HALF // GROUP
-LAGS = ((0, 3, 6, 9, 15, 20, 25, 29, 33), (0, 3, 5, 8, 14, 19, 24, 29, 33))
-SEQUENCE = ((8, 0), (7, 1), (4, 1), (6, 0), (1, 1), (0, 0), (4, 0), (3, 1), (1, 0), (0, 1), (2, 0), (6, 1), (5, 1), (2, 1), (5, 0), (7, 0), (8, 1), (3, 0))
+LAGS = ((0, 3, 6, 8, 15, 21, 24, 29, 38), (0, 3, 7, 10, 16, 21, 25, 29, 42))
+SEQUENCE = ((7, 0), (8, 1), (8, 0), (6, 1), (4, 1), (5, 0), (0, 0), (3, 1), (2, 0), (2, 1), (1, 0), (6, 0), (7, 1), (5, 1), (3, 0), (0, 1), (4, 0), (1, 1))
 STEPS = PIECES + max(map(max, LAGS))
 FIRST_ADAM = min(lags[4] for lags in LAGS)
 LAST_ADAM = max(lags[4] for lags in LAGS) + PIECES - 1

time: 182 us -> 182 us (level)
  no operation moved by 1% of the time
where the time goes in v10:
time: 182 us
  Pallas kernels  181 us (99%)
    pallas_call x1, Pallas kernels, local_step(): pl.pallas_call(big_kernel, out_shape=(pltpu.VMEM((2, 2, 16, HALF, LANES),...  174 us
    pallas_call x1, Pallas kernels, local_step(): pl.pallas_call(place_kernel, out_shape=[jax.ShapeDtypeStruct((n, LANES),...  7.59 us

profile of v10, /device:TPU:0, one launch (start us, length us, event | category | flops | bytes accessed | tf_op | source)
XLA Modules:
  0.0 181.9 jit_solution(5637604580135399793)
XLA Ops:
  0.6 173.7 %reduce_adam_gather.1 = (bf16[2,2,16,928,128]{4,3,2,1,0:T(8,128)(2,1)S(1)}, f32[3,1928,128]{2,1,0:T(8,128)S(1)}) custom-call(f32[32768,128]{1,0:T(8,128)} %bitcast.39, f32[8192,128]{1,0:T(8,128)} %bitcast.40, f32[8192,128]{1,0:T(8,128)} %bitcast.41, f32[8192,128]{1,0:T(8,128)} %bitcast.42, f32[208,128]{1,0:T(8,128)} %bitcast.43, f32[230208]{0:T(1024)} %m_in.1, ...), custom_call_target="tpu_custom_call" | custom-call | tf_op jit(solution)/shard_map/reduce_adam_gather/pallas_call | solution.py:509
  174.3 7.6 %place.1 = (bf16[32768,128]{1,0:T(8,128)(2,1)}, bf16[8192,128]{1,0:T(8,128)(2,1)}, bf16[8192,128]{1,0:T(8,128)(2,1)}, bf16[8192,128]{1,0:T(8,128)(2,1)}, bf16[20...) custom-call(bf16[2,2,16,928,128]{4,3,2,1,0:T(8,128)(2,1)S(1)} %get-t, ...), custom_call_target="tpu_custom_call" | custom-call | tf_op jit(solution)/shard_map/place/pallas_call | solution.py:519

commit v11 on v10

--- a/solution.py
+++ b/solution.py
@@ -51,8 +51,8 @@
 
 LOAD = bounds(LOADS)
 PIECES = HALF // GROUP
-LAGS = ((0, 3, 6, 8, 15, 21, 24, 29, 38), (0, 3, 7, 10, 16, 21, 25, 29, 42))
-SEQUENCE = ((7, 0), (8, 1), (8, 0), (6, 1), (4, 1), (5, 0), (0, 0), (3, 1), (2, 0), (2, 1), (1, 0), (6, 0), (7, 1), (5, 1), (3, 0), (0, 1), (4, 0), (1, 1))
+LAGS = ((0, 2, 5, 8, 14, 20, 23, 27, 33), (0, 2, 5, 7, 14, 19, 22, 27, 33))
+SEQUENCE = ((4, 1), (6, 0), (5, 0), (3, 0), (0, 0), (5, 1), (0, 1), (2, 1), (6, 1), (2, 0), (1, 0), (7, 1), (4, 0), (3, 1), (1, 1), (8, 0), (8, 1), (7, 0))
 STEPS = PIECES + max(map(max, LAGS))
 FIRST_ADAM = min(lags[4] for lags in LAGS)
 LAST_ADAM = max(lags[4] for lags in LAGS) + PIECES - 1

time: 182 us -> 182 us (level)
  no operation moved by 1% of the time
where the time goes in v11:
time: 182 us; the launch traced here: 181 us
  Pallas kernels  181 us (99%)
    pallas_call x1, Pallas kernels, local_step(): pl.pallas_call(big_kernel, out_shape=(pltpu.VMEM((2, 2, 16, HALF, LANES),...  173 us
    pallas_call x1, Pallas kernels, local_step(): pl.pallas_call(place_kernel, out_shape=[jax.ShapeDtypeStruct((n, LANES),...  7.59 us

profile of v11, /device:TPU:0, one launch (start us, length us, event | category | flops | bytes accessed | tf_op | source)
XLA Modules:
  0.0 181.5 jit_solution(15488009322672099089)
XLA Ops:
  0.6 173.3 %reduce_adam_gather.1 = (bf16[2,2,16,928,128]{4,3,2,1,0:T(8,128)(2,1)S(1)}, f32[3,1928,128]{2,1,0:T(8,128)S(1)}) custom-call(f32[32768,128]{1,0:T(8,128)} %bitcast.39, f32[8192,128]{1,0:T(8,128)} %bitcast.40, f32[8192,128]{1,0:T(8,128)} %bitcast.41, f32[8192,128]{1,0:T(8,128)} %bitcast.42, f32[208,128]{1,0:T(8,128)} %bitcast.43, f32[230208]{0:T(1024)} %m_in.1, ...), custom_call_target="tpu_custom_call" | custom-call | tf_op jit(solution)/shard_map/reduce_adam_gather/pallas_call | solution.py:509
  173.9 7.6 %place.1 = (bf16[32768,128]{1,0:T(8,128)(2,1)}, bf16[8192,128]{1,0:T(8,128)(2,1)}, bf16[8192,128]{1,0:T(8,128)(2,1)}, bf16[8192,128]{1,0:T(8,128)(2,1)}, bf16[20...) custom-call(bf16[2,2,16,928,128]{4,3,2,1,0:T(8,128)(2,1)S(1)} %get-t, ...), custom_call_target="tpu_custom_call" | custom-call | tf_op jit(solution)/shard_map/place/pallas_call | solution.py:519
